TPU v7x, 256 devices: a whole 4x4x8 slice. The times are simulated.
256 devices in a mesh: seq: 16 (over z, x_lo), head: 16 (over y, x_hi, core).
Axes of the slice: x: 4 (x_hi: 2, x_lo: 2; x = x_hi * 2 + x_lo), y: 4, z: 8, core: 2. Of those that a mesh axis runs over, the one named last changes fastest.
Arguments:
- queries: bfloat16 [8192, 6144], P('seq', 'head'), may hold values from -10 to 10
- keys: bfloat16 [8192, 6144], P('seq', 'head'), may hold values from -10 to 10
- values: bfloat16 [8192, 6144], P('seq', 'head'), may hold values from -6 to 6
- frame_of_block: int32 [32], P('seq'), may hold values from 0 to 15, never falling along the last dimension, each value on 1 to 4 neighbouring positions
- pair_mask: int32 [32, 32], P('seq'), may hold values 0 or 1
- w_out: bfloat16 [6144, 6144], P('head', 'seq'), may hold values from -0.4375 to 0.4375
Outputs:
- projected: bfloat16 [8192, 6144], P('seq', 'head')
Inputs may be any that keep to these rules, and one draw needn't show every extreme that they name: `frame_of_block`: frame ids never fall along the blocks, every frame spans 1 to 4 consecutive blocks.
All inputs are finite; a program needn't handle non-finite values. No bound on the sum of `pair_mask` on one device may be relied on, other than what follows from the above.
Results may differ from a plain program's by a relative error of at most 0.015.
Values may be sent and summed in bfloat16 or wider, within the bound.
A program may use at most 192 MiB of HBM per device.

v0:
```python
import math

import jax
import jax.numpy as jnp
from jax import lax
from jax.sharding import Mesh
from jax.sharding import PartitionSpec as P

HD = 128
BLK = 256
SEQ = ("seq_0", "seq_1")


def as_sent(shard):
    return jax.tree.map(lambda a: a.astype(jnp.bfloat16) if a.dtype == jnp.float32 else a, shard)


def from_behind(value, axis, steps):
    count = lax.axis_size(axis)
    pairs = [(source, (source + steps) % count) for source in range(count)]
    return lax.ppermute(value, axis, pairs)


def whole_of(shard, axes, dim):
    out = shard
    for number in range(len(axes) - 1, -1, -1):
        out = lax.all_gather(out, axes[number], axis=dim, tiled=True)
    return out


def body(queries, keys, values, frame_of_block, pair_mask, w_out):
    tok = queries.shape[0]
    heads_here = queries.shape[1] // HD
    count_blocks = pair_mask.shape[1]
    scale = 1.0 / math.sqrt(HD)
    key_span = 512
    q_heads = queries.reshape(tok, heads_here, HD)
    q_frame = jnp.repeat(frame_of_block, BLK)
    mask_rows = jnp.repeat(pair_mask.astype(jnp.float32), BLK, axis=0)
    block_ids = jnp.arange(count_blocks, dtype=jnp.int32)

    def update(state, k_rows, v_rows, allowed):
        peak, total, accum = state
        k_heads = k_rows.reshape(k_rows.shape[0], heads_here, HD)
        v_heads = v_rows.reshape(v_rows.shape[0], heads_here, HD)
        score = (
            jnp.einsum("qhd,khd->hqk", q_heads, k_heads, preferred_element_type=jnp.float32) * scale
        )
        score = jnp.where(allowed[None], score, -1e30)
        new_peak = jnp.maximum(peak, jnp.max(score, axis=2))
        weight = jnp.where(allowed[None], jnp.exp(score - new_peak[:, :, None]), 0.0)
        factor = jnp.exp(peak - new_peak)
        new_total = total * factor + jnp.sum(weight, axis=2)
        added = jnp.einsum(
            "hqk,khd->qhd", weight.astype(jnp.bfloat16), v_heads, preferred_element_type=jnp.float32
        )
        new_accum = accum * factor.T[:, :, None] + added
        return (new_peak, new_total, new_accum)

    def attend_block(state, k_rows, v_rows, k_frame, start):
        count = k_rows.shape[0]
        k_block = (start + jnp.arange(count, dtype=jnp.int32)) // BLK
        one_hot = (block_ids[:, None] == k_block[None, :]).astype(jnp.float32)
        link = jnp.dot(mask_rows, one_hot, preferred_element_type=jnp.float32)
        same = k_frame[None, :] == q_frame[:, None]
        allowed = (k_frame[None, :] <= q_frame[:, None]) & ((link > 0.5) | same)
        return update(state, k_rows, v_rows, allowed)

    def visit(state, piece, start):
        k_rows, v_rows, k_frame = piece
        count = k_rows.shape[0]
        return attend_block(state, k_rows, v_rows, k_frame, start)

    initial = (
        jnp.full((heads_here, tok), -1e30, jnp.float32),
        jnp.zeros((heads_here, tok), jnp.float32),
        jnp.zeros((tok, heads_here, HD), jnp.float32),
    )
    k_frame_local = jnp.repeat(frame_of_block, BLK)
    cycle_size = lax.axis_size(SEQ)
    position = lax.axis_index(SEQ)

    def turn(step, pair):
        state_now, held = pair
        anchor = (position - step) % cycle_size
        state_now = visit(state_now, held, anchor * tok)
        held = jax.tree.map(
            lambda part, own: part.astype(own.dtype), from_behind(as_sent(held), SEQ, 1), held
        )
        return (state_now, held)

    state, held = lax.fori_loop(0, cycle_size - 1, turn, (initial, (keys, values, k_frame_local)))
    anchor = (position - (cycle_size - 1)) % cycle_size
    state = visit(state, held, anchor * tok)
    peak, total, accum = state
    attn = (accum / total.T[:, :, None]).reshape(tok, heads_here * HD).astype(jnp.bfloat16)
    wide_rows = whole_of(w_out, SEQ, 1)
    own_columns = lax.all_to_all(wide_rows, "head", split_axis=1, concat_axis=0, tiled=True)
    full_attn = lax.all_gather(attn, "head", axis=1, tiled=True)
    return jnp.dot(full_attn, own_columns, preferred_element_type=jnp.float32).astype(jnp.bfloat16)


def solution(mesh):
    torus = Mesh(mesh.devices.reshape(8, 2, mesh.shape["head"]), ("seq_0", "seq_1", "head"))
    return jax.shard_map(
        body,
        mesh=torus,
        in_specs=(
            P(SEQ, "head"),
            P(SEQ, "head"),
            P(SEQ, "head"),
            P(SEQ),
            P(SEQ, None),
            P("head", SEQ),
        ),
        out_specs=P(SEQ, "head"),
        check_vma=False,
    )
```

profile of v0, /device:TPU:27, one launch (start us, length us, event | category | flops | bytes accessed | tf_op | source)
XLA Modules:
  0.0 457.7 jit_solution(13363778716746765918)
XLA Ops:
  7.8 8.7 %all_gather.10 = bf16[384,768]{0,1:T(8,128)(2,1)} all-gather(bf16[384,384]{0,1:T(8,128)(2,1)S(1)} %copy.36), channel_id=1, replica_groups=mesh['seq_0'=8,'seq_1'=2,'head'=16] {'seq_1'}, dimensions={1}, use_global_device_ids=true | all-gather | bytes 884736 | tf_op jit(solution)/shard_map/all_gather | solution.py:27
  19.8 311.7 %while.26 = (s32[]{:T(128)}, f32[3,512]{1,0:T(4,128)S(1)}, f32[3,512]{1,0:T(4,128)S(1)}, f32[512,3,128]{2,0,1:T(8,128)S(1)}, bf16[512,384]{0,1:T(8,128)(2,1)S(1)...) while((s32[]{:T(128)}, f32[3,512]{1,0:T(4,128)S(1)}, ...), condition=%wide.region_3.4_spmd.clone, body=%wide.region_0.3_spmd.clone.sunk | while | flops 431604736 | bytes 18147880 | solution.py:92
  19.8 1.7 collective-permute-start.2
  22.9 1.7 collective-permute-start.1
  26.0 1.5 fusion.96
  28.3 2.3 collective-permute-done
  30.5 13.8 %collective-permute-done.1 = bf16[512,384]{0,1:T(8,128)(2,1)S(1)} collective-permute-done((bf16[512,384]{0,1:T(8,128)(2,1)S(1)}, bf16[512,384]{0,1:T(8,128)(2,1)S(1)}, u32[]{:S(2)}, u32[]{:S(2)}) %collective-permute-start.1) | collective-permute-done | bytes 393248 | tf_op jit(solution)/shard_map/while/body/eval_jaxpr/ppermute | solution.py:21
  44.4 3.1 collective-permute-start.2
  47.7 3.2 collective-permute-start.1
  52.3 1.5 fusion.96
  54.6 8.8 %collective-permute-done = bf16[512,384]{0,1:T(8,128)(2,1)S(1)} collective-permute-done((bf16[512,384]{0,1:T(8,128)(2,1)S(1)}, bf16[512,384]{0,1:T(8,128)(2,1)S(1)}, u32[]{:S(2)}, u32[]{:S(2)}) %collective-permute-start) | collective-permute-done | bytes 393248 | tf_op jit(solution)/shard_map/while/body/eval_jaxpr/ppermute | solution.py:21
  63.4 16.9 %collective-permute-done.1 = bf16[512,384]{0,1:T(8,128)(2,1)S(1)} collective-permute-done((bf16[512,384]{0,1:T(8,128)(2,1)S(1)}, bf16[512,384]{0,1:T(8,128)(2,1)S(1)}, u32[]{:S(2)}, u32[]{:S(2)}) %collective-permute-start.1) | collective-permute-done | bytes 393248 | tf_op jit(solution)/shard_map/while/body/eval_jaxpr/ppermute | solution.py:21
  80.3 3.1 collective-permute-start.2
  83.7 3.2 collective-permute-start.1
  90.6 8.9 %collective-permute-done = bf16[512,384]{0,1:T(8,128)(2,1)S(1)} collective-permute-done((bf16[512,384]{0,1:T(8,128)(2,1)S(1)}, bf16[512,384]{0,1:T(8,128)(2,1)S(1)}, u32[]{:S(2)}, u32[]{:S(2)}) %collective-permute-start) | collective-permute-done | bytes 393248 | tf_op jit(solution)/shard_map/while/body/eval_jaxpr/ppermute | solution.py:21
  99.5 15.9 %collective-permute-done.1 = bf16[512,384]{0,1:T(8,128)(2,1)S(1)} collective-permute-done((bf16[512,384]{0,1:T(8,128)(2,1)S(1)}, bf16[512,384]{0,1:T(8,128)(2,1)S(1)}, u32[]{:S(2)}, u32[]{:S(2)}) %collective-permute-start.1) | collective-permute-done | bytes 393248 | tf_op jit(solution)/shard_map/while/body/eval_jaxpr/ppermute | solution.py:21
  115.4 3.1 collective-permute-start.2
  118.7 2.5 collective-permute-start.1
  122.6 1.5 fusion.96
  124.9 2.4 collective-permute-done
  127.3 8.4 %collective-permute-done.1 = bf16[512,384]{0,1:T(8,128)(2,1)S(1)} collective-permute-done((bf16[512,384]{0,1:T(8,128)(2,1)S(1)}, bf16[512,384]{0,1:T(8,128)(2,1)S(1)}, u32[]{:S(2)}, u32[]{:S(2)}) %collective-permute-start.1) | collective-permute-done | bytes 393248 | tf_op jit(solution)/shard_map/while/body/eval_jaxpr/ppermute | solution.py:21
  141.5 4.1 collective-permute-done
  145.6 8.4 %collective-permute-done.1 = bf16[512,384]{0,1:T(8,128)(2,1)S(1)} collective-permute-done((bf16[512,384]{0,1:T(8,128)(2,1)S(1)}, bf16[512,384]{0,1:T(8,128)(2,1)S(1)}, u32[]{:S(2)}, u32[]{:S(2)}) %collective-permute-start.1) | collective-permute-done | bytes 393248 | tf_op jit(solution)/shard_map/while/body/eval_jaxpr/ppermute | solution.py:21
  159.3 3.3 collective-permute-done
  162.6 8.5 %collective-permute-done.1 = bf16[512,384]{0,1:T(8,128)(2,1)S(1)} collective-permute-done((bf16[512,384]{0,1:T(8,128)(2,1)S(1)}, bf16[512,384]{0,1:T(8,128)(2,1)S(1)}, u32[]{:S(2)}, u32[]{:S(2)}) %collective-permute-start.1) | collective-permute-done | bytes 393248 | tf_op jit(solution)/shard_map/while/body/eval_jaxpr/ppermute | solution.py:21
  173.5 1.5 fusion.96
  175.8 3.8 collective-permute-done
  179.6 7.6 %collective-permute-done.1 = bf16[512,384]{0,1:T(8,128)(2,1)S(1)} collective-permute-done((bf16[512,384]{0,1:T(8,128)(2,1)S(1)}, bf16[512,384]{0,1:T(8,128)(2,1)S(1)}, u32[]{:S(2)}, u32[]{:S(2)}) %collective-permute-start.1) | collective-permute-done | bytes 393248 | tf_op jit(solution)/shard_map/while/body/eval_jaxpr/ppermute | solution.py:21
  189.5 1.5 fusion.96
  191.8 4.7 %collective-permute-done = bf16[512,384]{0,1:T(8,128)(2,1)S(1)} collective-permute-done((bf16[512,384]{0,1:T(8,128)(2,1)S(1)}, bf16[512,384]{0,1:T(8,128)(2,1)S(1)}, u32[]{:S(2)}, u32[]{:S(2)}) %collective-permute-start) | collective-permute-done | bytes 393248 | tf_op jit(solution)/shard_map/while/body/eval_jaxpr/ppermute | solution.py:21
  196.5 6.8 %collective-permute-done.1 = bf16[512,384]{0,1:T(8,128)(2,1)S(1)} collective-permute-done((bf16[512,384]{0,1:T(8,128)(2,1)S(1)}, bf16[512,384]{0,1:T(8,128)(2,1)S(1)}, u32[]{:S(2)}, u32[]{:S(2)}) %collective-permute-start.1) | collective-permute-done | bytes 393248 | tf_op jit(solution)/shard_map/while/body/eval_jaxpr/ppermute | solution.py:21
  205.6 1.5 fusion.96
  207.9 5.5 %collective-permute-done = bf16[512,384]{0,1:T(8,128)(2,1)S(1)} collective-permute-done((bf16[512,384]{0,1:T(8,128)(2,1)S(1)}, bf16[512,384]{0,1:T(8,128)(2,1)S(1)}, u32[]{:S(2)}, u32[]{:S(2)}) %collective-permute-start) | collective-permute-done | bytes 393248 | tf_op jit(solution)/shard_map/while/body/eval_jaxpr/ppermute | solution.py:21
  213.4 5.9 %collective-permute-done.1 = bf16[512,384]{0,1:T(8,128)(2,1)S(1)} collective-permute-done((bf16[512,384]{0,1:T(8,128)(2,1)S(1)}, bf16[512,384]{0,1:T(8,128)(2,1)S(1)}, u32[]{:S(2)}, u32[]{:S(2)}) %collective-permute-start.1) | collective-permute-done | bytes 393248 | tf_op jit(solution)/shard_map/while/body/eval_jaxpr/ppermute | solution.py:21
  222.0 1.5 fusion.96
  224.3 6.0 %collective-permute-done = bf16[512,384]{0,1:T(8,128)(2,1)S(1)} collective-permute-done((bf16[512,384]{0,1:T(8,128)(2,1)S(1)}, bf16[512,384]{0,1:T(8,128)(2,1)S(1)}, u32[]{:S(2)}, u32[]{:S(2)}) %collective-permute-start) | collective-permute-done | bytes 393248 | tf_op jit(solution)/shard_map/while/body/eval_jaxpr/ppermute | solution.py:21
  230.3 5.1 %collective-permute-done.1 = bf16[512,384]{0,1:T(8,128)(2,1)S(1)} collective-permute-done((bf16[512,384]{0,1:T(8,128)(2,1)S(1)}, bf16[512,384]{0,1:T(8,128)(2,1)S(1)}, u32[]{:S(2)}, u32[]{:S(2)}) %collective-permute-start.1) | collective-permute-done | bytes 393248 | tf_op jit(solution)/shard_map/while/body/eval_jaxpr/ppermute | solution.py:21
  235.6 2.3 collective-permute-start.1
  239.3 1.5 fusion.96
  241.6 5.6 %collective-permute-done = bf16[512,384]{0,1:T(8,128)(2,1)S(1)} collective-permute-done((bf16[512,384]{0,1:T(8,128)(2,1)S(1)}, bf16[512,384]{0,1:T(8,128)(2,1)S(1)}, u32[]{:S(2)}, u32[]{:S(2)}) %collective-permute-start) | collective-permute-done | bytes 393248 | tf_op jit(solution)/shard_map/while/body/eval_jaxpr/ppermute | solution.py:21
  247.2 4.2 collective-permute-done.1
  251.6 2.3 collective-permute-start
  253.9 2.7 collective-permute-start.1
  258.0 1.5 fusion.96
  260.3 4.3 collective-permute-done
  264.6 4.2 collective-permute-done.1
  268.8 3.0 collective-permute-start.2
  271.9 2.0 collective-permute-start
  278.9 4.1 collective-permute-done
  283.1 7.5 %collective-permute-done.1 = bf16[512,384]{0,1:T(8,128)(2,1)S(1)} collective-permute-done((bf16[512,384]{0,1:T(8,128)(2,1)S(1)}, bf16[512,384]{0,1:T(8,128)(2,1)S(1)}, u32[]{:S(2)}, u32[]{:S(2)}) %collective-permute-start.1) | collective-permute-done | bytes 393248 | tf_op jit(solution)/shard_map/while/body/eval_jaxpr/ppermute | solution.py:21
  290.6 2.8 collective-permute-start.2
  293.6 2.2 collective-permute-start.1
  297.2 1.5 fusion.96
  299.5 4.3 collective-permute-done
  303.8 8.4 %collective-permute-done.1 = bf16[512,384]{0,1:T(8,128)(2,1)S(1)} collective-permute-done((bf16[512,384]{0,1:T(8,128)(2,1)S(1)}, bf16[512,384]{0,1:T(8,128)(2,1)S(1)}, u32[]{:S(2)}, u32[]{:S(2)}) %collective-permute-start.1) | collective-permute-done | bytes 393248 | tf_op jit(solution)/shard_map/while/body/eval_jaxpr/ppermute | solution.py:21
  313.5 1.6 collective-permute-start
  315.1 2.2 collective-permute-start.1
  321.1 2.1 collective-permute-done
  323.1 8.4 %collective-permute-done.1 = bf16[512,384]{0,1:T(8,128)(2,1)S(1)} collective-permute-done((bf16[512,384]{0,1:T(8,128)(2,1)S(1)}, bf16[512,384]{0,1:T(8,128)(2,1)S(1)}, u32[]{:S(2)}, u32[]{:S(2)}) %collective-permute-start.1) | collective-permute-done | bytes 393248 | tf_op jit(solution)/shard_map/while/body/eval_jaxpr/ppermute | solution.py:21
  334.0 1.8 fusion.50
  335.8 83.1 %all_to_all.19 = bf16[384,16,384]{0,2,1:T(8,128)(2,1)} all-to-all(bf16[384,16,384]{0,2,1:T(8,128)(2,1)} %bitcast.106), channel_id=1, replica_groups=mesh['seq_0'=8,'seq_1'=2,'head'=16] {'head'}, dimensions={1} | all-to-all | bytes 9437184 | tf_op jit(solution)/shard_map/all_to_all | solution.py:98
  418.9 6.7 %copy.37 = bf16[16,384,384]{2,1,0:T(8,128)(2,1)} copy(bf16[16,384,384]{1,2,0:T(8,128)(2,1)} %bitcast.103) | data formatting | bytes 9437184 | tf_op jit(solution)/shard_map/all_to_all | solution.py:98
  425.6 16.9 %all-gather.3.cloned.1.call-done = bf16[512,6144]{0,1:T(8,128)(2,1)} async-done(((bf16[512,384]{0,1:T(8,128)(2,1)}), bf16[512,6144]{0,1:T(8,128)(2,1)}) %all-gather.3.cloned.1.call-update) | async-done | bytes 6291472 | tf_op jit(solution)/shard_map/all_gather | solution.py:99
  442.6 8.3 %convolution_convert_fusion = bf16[512,384]{1,0:T(8,128)(2,1)} fusion(bf16[512,6144]{0,1:T(8,128)(2,1)} %all-gather.3.cloned.1.call-done, bf16[6144,384]{1,0:T(8,128)(2,1)} %bitcast.101), kind=kOutput, calls=%fused_computation.48 | convolution fusion | flops 2416115712 | bytes 11403264 | tf_op jit(solution)/shard_map/dot_general | solution.py:100
  (274 shorter events, 59.9 us)
Async XLA Ops:
  6.5 13.3 %copy-start.2 = (s32[2]{0:T(128)S(1)}, s32[2]{0:T(128)}, u32[]{:S(2)}) copy-start(s32[2]{0:T(128)} %param.11) | copy-start | bytes 28
  6.5 12.9 %copy-start = (bf16[512,384]{1,0:T(8,128)(2,1)S(1)}, bf16[512,384]{1,0:T(8,128)(2,1)}, u32[]{:S(2)}) copy-start(bf16[512,384]{1,0:T(8,128)(2,1)} %param.9) | copy-start | bytes 1179652
  6.5 13.1 %copy-start.1 = (bf16[512,384]{1,0:T(8,128)(2,1)S(1)}, bf16[512,384]{1,0:T(8,128)(2,1)}, u32[]{:S(2)}) copy-start(bf16[512,384]{1,0:T(8,128)(2,1)} %param.10) | copy-start | bytes 1179652
  6.5 329.3 %all-gather.5.cloned.1.call-start = ((), (), s32[]{:S(2)}) async-start(), calls=%async_computation.2 | async-start | bytes 5308416 | tf_op jit(solution)/shard_map/all_gather | solution.py:27
  16.5 426.1 %all-gather.3.cloned.1.call-start = ((), (), s32[]{:S(2)}) async-start(), calls=%async_computation.1 | async-start | bytes 6684672 | tf_op jit(solution)/shard_map/all_gather | solution.py:99
  19.8 8.4 %collective-permute-start.2 = (s32[512]{0:T(512)S(1)}, s32[512]{0:T(512)S(1)}, u32[]{:S(2)}, u32[]{:S(2)}) collective-permute-start(s32[512]{0:T(512)S(1)} %copy.61), channel_id=1, source_target_pairs={{0,16},{16,32},{32,48},{48,64},{64,80},{80,96},{96,112},{112,128},... | collective-permute-start | bytes 6152 | tf_op jit(solution)/shard_map/while/body/eval_jaxpr/ppermute | solution.py:21
  21.6 9.0 %collective-permute-start = (bf16[512,384]{0,1:T(8,128)(2,1)S(1)}, bf16[512,384]{0,1:T(8,128)(2,1)S(1)}, u32[]{:S(2)}, u32[]{:S(2)}) collective-permute-start(bf16[512,384]{0,1:T(8,128)(2,1)S(1)} %copy.59), channel_id=1, source_target_pairs={{0,16},{16,32},{32,48},{48,64},{64,80},{80,96},{96,112},{112,128},... | collective-permute-start | bytes 1179656 | tf_op jit(solution)/shard_map/while/body/eval_jaxpr/ppermute | solution.py:21
  22.9 21.5 %collective-permute-start.1 = (bf16[512,384]{0,1:T(8,128)(2,1)S(1)}, bf16[512,384]{0,1:T(8,128)(2,1)S(1)}, u32[]{:S(2)}, u32[]{:S(2)}) collective-permute-start(bf16[512,384]{0,1:T(8,128)(2,1)S(1)} %copy.60), channel_id=1, source_target_pairs={{0,16},{16,32},{32,48},{48,64},{64,80},{80,96},{96,112},{112,128},... | collective-permute-start | bytes 1179656 | tf_op jit(solution)/shard_map/while/body/eval_jaxpr/ppermute | solution.py:21
  44.4 10.2 %collective-permute-start.2 = (s32[512]{0:T(512)S(1)}, s32[512]{0:T(512)S(1)}, u32[]{:S(2)}, u32[]{:S(2)}) collective-permute-start(s32[512]{0:T(512)S(1)} %copy.61), channel_id=1, source_target_pairs={{0,16},{16,32},{32,48},{48,64},{64,80},{80,96},{96,112},{112,128},... | collective-permute-start | bytes 6152 | tf_op jit(solution)/shard_map/while/body/eval_jaxpr/ppermute | solution.py:21
  47.5 15.9 %collective-permute-start = (bf16[512,384]{0,1:T(8,128)(2,1)S(1)}, bf16[512,384]{0,1:T(8,128)(2,1)S(1)}, u32[]{:S(2)}, u32[]{:S(2)}) collective-permute-start(bf16[512,384]{0,1:T(8,128)(2,1)S(1)} %copy.59), channel_id=1, source_target_pairs={{0,16},{16,32},{32,48},{48,64},{64,80},{80,96},{96,112},{112,128},... | collective-permute-start | bytes 1179656 | tf_op jit(solution)/shard_map/while/body/eval_jaxpr/ppermute | solution.py:21
  47.7 32.6 %collective-permute-start.1 = (bf16[512,384]{0,1:T(8,128)(2,1)S(1)}, bf16[512,384]{0,1:T(8,128)(2,1)S(1)}, u32[]{:S(2)}, u32[]{:S(2)}) collective-permute-start(bf16[512,384]{0,1:T(8,128)(2,1)S(1)} %copy.60), channel_id=1, source_target_pairs={{0,16},{16,32},{32,48},{48,64},{64,80},{80,96},{96,112},{112,128},... | collective-permute-start | bytes 1179656 | tf_op jit(solution)/shard_map/while/body/eval_jaxpr/ppermute | solution.py:21
  80.3 10.3 %collective-permute-start.2 = (s32[512]{0:T(512)S(1)}, s32[512]{0:T(512)S(1)}, u32[]{:S(2)}, u32[]{:S(2)}) collective-permute-start(s32[512]{0:T(512)S(1)} %copy.61), channel_id=1, source_target_pairs={{0,16},{16,32},{32,48},{48,64},{64,80},{80,96},{96,112},{112,128},... | collective-permute-start | bytes 6152 | tf_op jit(solution)/shard_map/while/body/eval_jaxpr/ppermute | solution.py:21
  83.4 16.1 %collective-permute-start = (bf16[512,384]{0,1:T(8,128)(2,1)S(1)}, bf16[512,384]{0,1:T(8,128)(2,1)S(1)}, u32[]{:S(2)}, u32[]{:S(2)}) collective-permute-start(bf16[512,384]{0,1:T(8,128)(2,1)S(1)} %copy.59), channel_id=1, source_target_pairs={{0,16},{16,32},{32,48},{48,64},{64,80},{80,96},{96,112},{112,128},... | collective-permute-start | bytes 1179656 | tf_op jit(solution)/shard_map/while/body/eval_jaxpr/ppermute | solution.py:21
  83.7 31.7 %collective-permute-start.1 = (bf16[512,384]{0,1:T(8,128)(2,1)S(1)}, bf16[512,384]{0,1:T(8,128)(2,1)S(1)}, u32[]{:S(2)}, u32[]{:S(2)}) collective-permute-start(bf16[512,384]{0,1:T(8,128)(2,1)S(1)} %copy.60), channel_id=1, source_target_pairs={{0,16},{16,32},{32,48},{48,64},{64,80},{80,96},{96,112},{112,128},... | collective-permute-start | bytes 1179656 | tf_op jit(solution)/shard_map/while/body/eval_jaxpr/ppermute | solution.py:21
  115.4 9.5 %collective-permute-start.2 = (s32[512]{0:T(512)S(1)}, s32[512]{0:T(512)S(1)}, u32[]{:S(2)}, u32[]{:S(2)}) collective-permute-start(s32[512]{0:T(512)S(1)} %copy.61), channel_id=1, source_target_pairs={{0,16},{16,32},{32,48},{48,64},{64,80},{80,96},{96,112},{112,128},... | collective-permute-start | bytes 6152 | tf_op jit(solution)/shard_map/while/body/eval_jaxpr/ppermute | solution.py:21
  118.5 8.7 %collective-permute-start = (bf16[512,384]{0,1:T(8,128)(2,1)S(1)}, bf16[512,384]{0,1:T(8,128)(2,1)S(1)}, u32[]{:S(2)}, u32[]{:S(2)}) collective-permute-start(bf16[512,384]{0,1:T(8,128)(2,1)S(1)} %copy.59), channel_id=1, source_target_pairs={{0,16},{16,32},{32,48},{48,64},{64,80},{80,96},{96,112},{112,128},... | collective-permute-start | bytes 1179656 | tf_op jit(solution)/shard_map/while/body/eval_jaxpr/ppermute | solution.py:21
  118.7 17.0 %collective-permute-start.1 = (bf16[512,384]{0,1:T(8,128)(2,1)S(1)}, bf16[512,384]{0,1:T(8,128)(2,1)S(1)}, u32[]{:S(2)}, u32[]{:S(2)}) collective-permute-start(bf16[512,384]{0,1:T(8,128)(2,1)S(1)} %copy.60), channel_id=1, source_target_pairs={{0,16},{16,32},{32,48},{48,64},{64,80},{80,96},{96,112},{112,128},... | collective-permute-start | bytes 1179656 | tf_op jit(solution)/shard_map/while/body/eval_jaxpr/ppermute | solution.py:21
  135.7 5.8 %collective-permute-start.2 = (s32[512]{0:T(512)S(1)}, s32[512]{0:T(512)S(1)}, u32[]{:S(2)}, u32[]{:S(2)}) collective-permute-start(s32[512]{0:T(512)S(1)} %copy.61), channel_id=1, source_target_pairs={{0,16},{16,32},{32,48},{48,64},{64,80},{80,96},{96,112},{112,128},... | collective-permute-start | bytes 6152 | tf_op jit(solution)/shard_map/while/body/eval_jaxpr/ppermute | solution.py:21
  135.7 9.8 %collective-permute-start = (bf16[512,384]{0,1:T(8,128)(2,1)S(1)}, bf16[512,384]{0,1:T(8,128)(2,1)S(1)}, u32[]{:S(2)}, u32[]{:S(2)}) collective-permute-start(bf16[512,384]{0,1:T(8,128)(2,1)S(1)} %copy.59), channel_id=1, source_target_pairs={{0,16},{16,32},{32,48},{48,64},{64,80},{80,96},{96,112},{112,128},... | collective-permute-start | bytes 1179656 | tf_op jit(solution)/shard_map/while/body/eval_jaxpr/ppermute | solution.py:21
  136.5 17.5 %collective-permute-start.1 = (bf16[512,384]{0,1:T(8,128)(2,1)S(1)}, bf16[512,384]{0,1:T(8,128)(2,1)S(1)}, u32[]{:S(2)}, u32[]{:S(2)}) collective-permute-start(bf16[512,384]{0,1:T(8,128)(2,1)S(1)} %copy.60), channel_id=1, source_target_pairs={{0,16},{16,32},{32,48},{48,64},{64,80},{80,96},{96,112},{112,128},... | collective-permute-start | bytes 1179656 | tf_op jit(solution)/shard_map/while/body/eval_jaxpr/ppermute | solution.py:21
  154.0 5.3 %collective-permute-start.2 = (s32[512]{0:T(512)S(1)}, s32[512]{0:T(512)S(1)}, u32[]{:S(2)}, u32[]{:S(2)}) collective-permute-start(s32[512]{0:T(512)S(1)} %copy.61), channel_id=1, source_target_pairs={{0,16},{16,32},{32,48},{48,64},{64,80},{80,96},{96,112},{112,128},... | collective-permute-start | bytes 6152 | tf_op jit(solution)/shard_map/while/body/eval_jaxpr/ppermute | solution.py:21
  154.0 8.5 %collective-permute-start = (bf16[512,384]{0,1:T(8,128)(2,1)S(1)}, bf16[512,384]{0,1:T(8,128)(2,1)S(1)}, u32[]{:S(2)}, u32[]{:S(2)}) collective-permute-start(bf16[512,384]{0,1:T(8,128)(2,1)S(1)} %copy.59), channel_id=1, source_target_pairs={{0,16},{16,32},{32,48},{48,64},{64,80},{80,96},{96,112},{112,128},... | collective-permute-start | bytes 1179656 | tf_op jit(solution)/shard_map/while/body/eval_jaxpr/ppermute | solution.py:21
  154.2 16.9 %collective-permute-start.1 = (bf16[512,384]{0,1:T(8,128)(2,1)S(1)}, bf16[512,384]{0,1:T(8,128)(2,1)S(1)}, u32[]{:S(2)}, u32[]{:S(2)}) collective-permute-start(bf16[512,384]{0,1:T(8,128)(2,1)S(1)} %copy.60), channel_id=1, source_target_pairs={{0,16},{16,32},{32,48},{48,64},{64,80},{80,96},{96,112},{112,128},... | collective-permute-start | bytes 1179656 | tf_op jit(solution)/shard_map/while/body/eval_jaxpr/ppermute | solution.py:21
  171.1 4.8 %collective-permute-start.2 = (s32[512]{0:T(512)S(1)}, s32[512]{0:T(512)S(1)}, u32[]{:S(2)}, u32[]{:S(2)}) collective-permute-start(s32[512]{0:T(512)S(1)} %copy.61), channel_id=1, source_target_pairs={{0,16},{16,32},{32,48},{48,64},{64,80},{80,96},{96,112},{112,128},... | collective-permute-start | bytes 6152 | tf_op jit(solution)/shard_map/while/body/eval_jaxpr/ppermute | solution.py:21
  171.1 8.5 %collective-permute-start = (bf16[512,384]{0,1:T(8,128)(2,1)S(1)}, bf16[512,384]{0,1:T(8,128)(2,1)S(1)}, u32[]{:S(2)}, u32[]{:S(2)}) collective-permute-start(bf16[512,384]{0,1:T(8,128)(2,1)S(1)} %copy.59), channel_id=1, source_target_pairs={{0,16},{16,32},{32,48},{48,64},{64,80},{80,96},{96,112},{112,128},... | collective-permute-start | bytes 1179656 | tf_op jit(solution)/shard_map/while/body/eval_jaxpr/ppermute | solution.py:21
  171.2 16.0 %collective-permute-start.1 = (bf16[512,384]{0,1:T(8,128)(2,1)S(1)}, bf16[512,384]{0,1:T(8,128)(2,1)S(1)}, u32[]{:S(2)}, u32[]{:S(2)}) collective-permute-start(bf16[512,384]{0,1:T(8,128)(2,1)S(1)} %copy.60), channel_id=1, source_target_pairs={{0,16},{16,32},{32,48},{48,64},{64,80},{80,96},{96,112},{112,128},... | collective-permute-start | bytes 1179656 | tf_op jit(solution)/shard_map/while/body/eval_jaxpr/ppermute | solution.py:21
  187.3 4.6 %collective-permute-start.2 = (s32[512]{0:T(512)S(1)}, s32[512]{0:T(512)S(1)}, u32[]{:S(2)}, u32[]{:S(2)}) collective-permute-start(s32[512]{0:T(512)S(1)} %copy.61), channel_id=1, source_target_pairs={{0,16},{16,32},{32,48},{48,64},{64,80},{80,96},{96,112},{112,128},... | collective-permute-start | bytes 6152 | tf_op jit(solution)/shard_map/while/body/eval_jaxpr/ppermute | solution.py:21
  187.3 9.2 %collective-permute-start = (bf16[512,384]{0,1:T(8,128)(2,1)S(1)}, bf16[512,384]{0,1:T(8,128)(2,1)S(1)}, u32[]{:S(2)}, u32[]{:S(2)}) collective-permute-start(bf16[512,384]{0,1:T(8,128)(2,1)S(1)} %copy.59), channel_id=1, source_target_pairs={{0,16},{16,32},{32,48},{48,64},{64,80},{80,96},{96,112},{112,128},... | collective-permute-start | bytes 1179656 | tf_op jit(solution)/shard_map/while/body/eval_jaxpr/ppermute | solution.py:21
  187.4 15.9 %collective-permute-start.1 = (bf16[512,384]{0,1:T(8,128)(2,1)S(1)}, bf16[512,384]{0,1:T(8,128)(2,1)S(1)}, u32[]{:S(2)}, u32[]{:S(2)}) collective-permute-start(bf16[512,384]{0,1:T(8,128)(2,1)S(1)} %copy.60), channel_id=1, source_target_pairs={{0,16},{16,32},{32,48},{48,64},{64,80},{80,96},{96,112},{112,128},... | collective-permute-start | bytes 1179656 | tf_op jit(solution)/shard_map/while/body/eval_jaxpr/ppermute | solution.py:21
  203.3 4.6 %collective-permute-start.2 = (s32[512]{0:T(512)S(1)}, s32[512]{0:T(512)S(1)}, u32[]{:S(2)}, u32[]{:S(2)}) collective-permute-start(s32[512]{0:T(512)S(1)} %copy.61), channel_id=1, source_target_pairs={{0,16},{16,32},{32,48},{48,64},{64,80},{80,96},{96,112},{112,128},... | collective-permute-start | bytes 6152 | tf_op jit(solution)/shard_map/while/body/eval_jaxpr/ppermute | solution.py:21
  203.3 10.1 %collective-permute-start = (bf16[512,384]{0,1:T(8,128)(2,1)S(1)}, bf16[512,384]{0,1:T(8,128)(2,1)S(1)}, u32[]{:S(2)}, u32[]{:S(2)}) collective-permute-start(bf16[512,384]{0,1:T(8,128)(2,1)S(1)} %copy.59), channel_id=1, source_target_pairs={{0,16},{16,32},{32,48},{48,64},{64,80},{80,96},{96,112},{112,128},... | collective-permute-start | bytes 1179656 | tf_op jit(solution)/shard_map/while/body/eval_jaxpr/ppermute | solution.py:21
  203.5 15.9 %collective-permute-start.1 = (bf16[512,384]{0,1:T(8,128)(2,1)S(1)}, bf16[512,384]{0,1:T(8,128)(2,1)S(1)}, u32[]{:S(2)}, u32[]{:S(2)}) collective-permute-start(bf16[512,384]{0,1:T(8,128)(2,1)S(1)} %copy.60), channel_id=1, source_target_pairs={{0,16},{16,32},{32,48},{48,64},{64,80},{80,96},{96,112},{112,128},... | collective-permute-start | bytes 1179656 | tf_op jit(solution)/shard_map/while/body/eval_jaxpr/ppermute | solution.py:21
  219.4 5.0 %collective-permute-start.2 = (s32[512]{0:T(512)S(1)}, s32[512]{0:T(512)S(1)}, u32[]{:S(2)}, u32[]{:S(2)}) collective-permute-start(s32[512]{0:T(512)S(1)} %copy.61), channel_id=1, source_target_pairs={{0,16},{16,32},{32,48},{48,64},{64,80},{80,96},{96,112},{112,128},... | collective-permute-start | bytes 6152 | tf_op jit(solution)/shard_map/while/body/eval_jaxpr/ppermute | solution.py:21
  219.4 10.9 %collective-permute-start = (bf16[512,384]{0,1:T(8,128)(2,1)S(1)}, bf16[512,384]{0,1:T(8,128)(2,1)S(1)}, u32[]{:S(2)}, u32[]{:S(2)}) collective-permute-start(bf16[512,384]{0,1:T(8,128)(2,1)S(1)} %copy.59), channel_id=1, source_target_pairs={{0,16},{16,32},{32,48},{48,64},{64,80},{80,96},{96,112},{112,128},... | collective-permute-start | bytes 1179656 | tf_op jit(solution)/shard_map/while/body/eval_jaxpr/ppermute | solution.py:21
  219.5 15.9 %collective-permute-start.1 = (bf16[512,384]{0,1:T(8,128)(2,1)S(1)}, bf16[512,384]{0,1:T(8,128)(2,1)S(1)}, u32[]{:S(2)}, u32[]{:S(2)}) collective-permute-start(bf16[512,384]{0,1:T(8,128)(2,1)S(1)} %copy.60), channel_id=1, source_target_pairs={{0,16},{16,32},{32,48},{48,64},{64,80},{80,96},{96,112},{112,128},... | collective-permute-start | bytes 1179656 | tf_op jit(solution)/shard_map/while/body/eval_jaxpr/ppermute | solution.py:21
  235.4 6.2 %collective-permute-start.2 = (s32[512]{0:T(512)S(1)}, s32[512]{0:T(512)S(1)}, u32[]{:S(2)}, u32[]{:S(2)}) collective-permute-start(s32[512]{0:T(512)S(1)} %copy.61), channel_id=1, source_target_pairs={{0,16},{16,32},{32,48},{48,64},{64,80},{80,96},{96,112},{112,128},... | collective-permute-start | bytes 6152 | tf_op jit(solution)/shard_map/while/body/eval_jaxpr/ppermute | solution.py:21
  235.4 11.8 %collective-permute-start = (bf16[512,384]{0,1:T(8,128)(2,1)S(1)}, bf16[512,384]{0,1:T(8,128)(2,1)S(1)}, u32[]{:S(2)}, u32[]{:S(2)}) collective-permute-start(bf16[512,384]{0,1:T(8,128)(2,1)S(1)} %copy.59), channel_id=1, source_target_pairs={{0,16},{16,32},{32,48},{48,64},{64,80},{80,96},{96,112},{112,128},... | collective-permute-start | bytes 1179656 | tf_op jit(solution)/shard_map/while/body/eval_jaxpr/ppermute | solution.py:21
  235.6 15.9 %collective-permute-start.1 = (bf16[512,384]{0,1:T(8,128)(2,1)S(1)}, bf16[512,384]{0,1:T(8,128)(2,1)S(1)}, u32[]{:S(2)}, u32[]{:S(2)}) collective-permute-start(bf16[512,384]{0,1:T(8,128)(2,1)S(1)} %copy.60), channel_id=1, source_target_pairs={{0,16},{16,32},{32,48},{48,64},{64,80},{80,96},{96,112},{112,128},... | collective-permute-start | bytes 1179656 | tf_op jit(solution)/shard_map/while/body/eval_jaxpr/ppermute | solution.py:21
  251.4 8.9 %collective-permute-start.2 = (s32[512]{0:T(512)S(1)}, s32[512]{0:T(512)S(1)}, u32[]{:S(2)}, u32[]{:S(2)}) collective-permute-start(s32[512]{0:T(512)S(1)} %copy.61), channel_id=1, source_target_pairs={{0,16},{16,32},{32,48},{48,64},{64,80},{80,96},{96,112},{112,128},... | collective-permute-start | bytes 6152 | tf_op jit(solution)/shard_map/while/body/eval_jaxpr/ppermute | solution.py:21
  251.6 13.0 %collective-permute-start = (bf16[512,384]{0,1:T(8,128)(2,1)S(1)}, bf16[512,384]{0,1:T(8,128)(2,1)S(1)}, u32[]{:S(2)}, u32[]{:S(2)}) collective-permute-start(bf16[512,384]{0,1:T(8,128)(2,1)S(1)} %copy.59), channel_id=1, source_target_pairs={{0,16},{16,32},{32,48},{48,64},{64,80},{80,96},{96,112},{112,128},... | collective-permute-start | bytes 1179656 | tf_op jit(solution)/shard_map/while/body/eval_jaxpr/ppermute | solution.py:21
  253.9 14.9 %collective-permute-start.1 = (bf16[512,384]{0,1:T(8,128)(2,1)S(1)}, bf16[512,384]{0,1:T(8,128)(2,1)S(1)}, u32[]{:S(2)}, u32[]{:S(2)}) collective-permute-start(bf16[512,384]{0,1:T(8,128)(2,1)S(1)} %copy.60), channel_id=1, source_target_pairs={{0,16},{16,32},{32,48},{48,64},{64,80},{80,96},{96,112},{112,128},... | collective-permute-start | bytes 1179656 | tf_op jit(solution)/shard_map/while/body/eval_jaxpr/ppermute | solution.py:21
  268.8 10.1 %collective-permute-start.2 = (s32[512]{0:T(512)S(1)}, s32[512]{0:T(512)S(1)}, u32[]{:S(2)}, u32[]{:S(2)}) collective-permute-start(s32[512]{0:T(512)S(1)} %copy.61), channel_id=1, source_target_pairs={{0,16},{16,32},{32,48},{48,64},{64,80},{80,96},{96,112},{112,128},... | collective-permute-start | bytes 6152 | tf_op jit(solution)/shard_map/while/body/eval_jaxpr/ppermute | solution.py:21
  271.9 11.2 %collective-permute-start = (bf16[512,384]{0,1:T(8,128)(2,1)S(1)}, bf16[512,384]{0,1:T(8,128)(2,1)S(1)}, u32[]{:S(2)}, u32[]{:S(2)}) collective-permute-start(bf16[512,384]{0,1:T(8,128)(2,1)S(1)} %copy.59), channel_id=1, source_target_pairs={{0,16},{16,32},{32,48},{48,64},{64,80},{80,96},{96,112},{112,128},... | collective-permute-start | bytes 1179656 | tf_op jit(solution)/shard_map/while/body/eval_jaxpr/ppermute | solution.py:21
  273.9 16.7 %collective-permute-start.1 = (bf16[512,384]{0,1:T(8,128)(2,1)S(1)}, bf16[512,384]{0,1:T(8,128)(2,1)S(1)}, u32[]{:S(2)}, u32[]{:S(2)}) collective-permute-start(bf16[512,384]{0,1:T(8,128)(2,1)S(1)} %copy.60), channel_id=1, source_target_pairs={{0,16},{16,32},{32,48},{48,64},{64,80},{80,96},{96,112},{112,128},... | collective-permute-start | bytes 1179656 | tf_op jit(solution)/shard_map/while/body/eval_jaxpr/ppermute | solution.py:21
  290.6 8.9 %collective-permute-start.2 = (s32[512]{0:T(512)S(1)}, s32[512]{0:T(512)S(1)}, u32[]{:S(2)}, u32[]{:S(2)}) collective-permute-start(s32[512]{0:T(512)S(1)} %copy.61), channel_id=1, source_target_pairs={{0,16},{16,32},{32,48},{48,64},{64,80},{80,96},{96,112},{112,128},... | collective-permute-start | bytes 6152 | tf_op jit(solution)/shard_map/while/body/eval_jaxpr/ppermute | solution.py:21
  293.4 10.4 %collective-permute-start = (bf16[512,384]{0,1:T(8,128)(2,1)S(1)}, bf16[512,384]{0,1:T(8,128)(2,1)S(1)}, u32[]{:S(2)}, u32[]{:S(2)}) collective-permute-start(bf16[512,384]{0,1:T(8,128)(2,1)S(1)} %copy.59), channel_id=1, source_target_pairs={{0,16},{16,32},{32,48},{48,64},{64,80},{80,96},{96,112},{112,128},... | collective-permute-start | bytes 1179656 | tf_op jit(solution)/shard_map/while/body/eval_jaxpr/ppermute | solution.py:21
  293.6 18.7 %collective-permute-start.1 = (bf16[512,384]{0,1:T(8,128)(2,1)S(1)}, bf16[512,384]{0,1:T(8,128)(2,1)S(1)}, u32[]{:S(2)}, u32[]{:S(2)}) collective-permute-start(bf16[512,384]{0,1:T(8,128)(2,1)S(1)} %copy.60), channel_id=1, source_target_pairs={{0,16},{16,32},{32,48},{48,64},{64,80},{80,96},{96,112},{112,128},... | collective-permute-start | bytes 1179656 | tf_op jit(solution)/shard_map/while/body/eval_jaxpr/ppermute | solution.py:21
  312.3 8.8 %collective-permute-start.2 = (s32[512]{0:T(512)S(1)}, s32[512]{0:T(512)S(1)}, u32[]{:S(2)}, u32[]{:S(2)}) collective-permute-start(s32[512]{0:T(512)S(1)} %copy.61), channel_id=1, source_target_pairs={{0,16},{16,32},{32,48},{48,64},{64,80},{80,96},{96,112},{112,128},... | collective-permute-start | bytes 6152 | tf_op jit(solution)/shard_map/while/body/eval_jaxpr/ppermute | solution.py:21
  313.5 9.6 %collective-permute-start = (bf16[512,384]{0,1:T(8,128)(2,1)S(1)}, bf16[512,384]{0,1:T(8,128)(2,1)S(1)}, u32[]{:S(2)}, u32[]{:S(2)}) collective-permute-start(bf16[512,384]{0,1:T(8,128)(2,1)S(1)} %copy.59), channel_id=1, source_target_pairs={{0,16},{16,32},{32,48},{48,64},{64,80},{80,96},{96,112},{112,128},... | collective-permute-start | bytes 1179656 | tf_op jit(solution)/shard_map/while/body/eval_jaxpr/ppermute | solution.py:21
  315.1 16.4 %collective-permute-start.1 = (bf16[512,384]{0,1:T(8,128)(2,1)S(1)}, bf16[512,384]{0,1:T(8,128)(2,1)S(1)}, u32[]{:S(2)}, u32[]{:S(2)}) collective-permute-start(bf16[512,384]{0,1:T(8,128)(2,1)S(1)} %copy.60), channel_id=1, source_target_pairs={{0,16},{16,32},{32,48},{48,64},{64,80},{80,96},{96,112},{112,128},... | collective-permute-start | bytes 1179656 | tf_op jit(solution)/shard_map/while/body/eval_jaxpr/ppermute | solution.py:21
Sparse Core Ops, SparseCore 0:
  16.6 100.5 all-gather.4
  335.9 106.6 all-gather.2
where the time goes:
time: 463 us; the launch traced here: 458 us
  waiting for transfers between devices  217 us (47%)
  blocking collectives  91.8 us (20%)
  starting transfers between devices  54.8 us (12%)
  matrix products  52 us (11%)
  other arithmetic  14.3 us (3%)
  between operations  13.6 us (3%)
  local copies, waits for them, and re-layouts  12.9 us (3%)
    ppermute x45, waiting for transfers between devices, from_behind(): return lax.ppermute(value, axis, pairs)  200 us
    all_to_all x1, blocking collectives, body(): lax.all_to_all(wide_rows, 'head', split_axis=1, concat_axis=0, tiled=True)  83.1 us
    ppermute x45, starting transfers between devices, from_behind(): return lax.ppermute(value, axis, pairs)  54.7 us
    dot_general x16, matrix products, update(): jnp.einsum('hqk,khd->qhd', weight.astype(jnp.bfloat16), v_heads, preferre...  23.7 us
    all_gather x1, waiting for transfers between devices, body(): full_attn = lax.all_gather(attn, 'head', axis=1, tiled=True)  16.9 us
    reduce_sum x16, other arithmetic, update(): new_total = total * factor + jnp.sum(weight, axis=2)  12.9 us
    dot_general x16, matrix products, update(): jnp.einsum('qhd,khd->hqk', q_heads, k_heads, preferred_element_type=jnp.f...  12.9 us
  transfers between devices with their start and end apart: 47, of which 31 were waited for; matrix products, arithmetic and copies ran while one was open for 15% of the time, Pallas kernels for 0%

commit v1 on v0

v1 whole, which is shorter than its diff:
```python
import functools
import math

import jax
import jax.numpy as jnp
from jax import lax
from jax.experimental import pallas as pl
from jax.experimental.pallas import tpu as pltpu
from jax.sharding import PartitionSpec as P

HD = 128
BLK = 256
MESH = pl.DeviceIdType.MESH
ANY = pl.ANY


def where_am_i():
    s, h = lax.axis_index("seq"), lax.axis_index("head")
    c = lax.rem(h, 2)
    return s, h - c, c, s // 2, lax.rem(s, 2)


def worker_of(s):
    low = lax.rem(s, 8)
    return jnp.where(low < 4, low, 7 - low)


def chunk_owner(kk, j):
    return (kk, 7 - kk, 8 + kk, 15 - kk)[j]


def remote(src, dst, send, recv, seq, head):
    return pltpu.make_async_remote_copy(
        src_ref=src, dst_ref=dst, send_sem=send, recv_sem=recv, device_id=(seq, head), device_id_type=MESH
    )


def spread_kernel(q, k, v, meta, qb, kv, mt, s_kv, s_q, s_m, s_f, r_z, r_x, r_s, r_q, r_m):
    s, hb, c, z, x = where_am_i()
    barrier = pltpu.get_barrier_semaphore()

    def greet(n, _):
        ps, pc = n // 2, lax.rem(n, 2)

        @pl.when(jnp.logical_not((ps == s) & (pc == c)))
        def _():
            pl.semaphore_signal(barrier, inc=1, device_id=(ps, hb + pc), device_id_type=MESH)

        return 0

    lax.fori_loop(0, 32, greet, 0)
    pl.semaphore_wait(barrier, 31)

    def put(src, dst, send, recv, seq, head, start):
        mine = (seq == s) & (head == hb + c)
        copy = remote(src, dst, send, recv, seq, head)
        if start:

            @pl.when(mine)
            def _():
                pltpu.make_async_copy(src, dst, recv).start()

            @pl.when(jnp.logical_not(mine))
            def _():
                copy.start()
        else:

            @pl.when(jnp.logical_not(mine))
            def _():
                copy.wait_send()

    def all_sends(start):
        for i in range(3):
            pz = 4 * c + i
            cols = pl.ds(i * HD, HD)
            for t, src in ((0, k), (1, v)):
                put(src.at[:, cols], kv.at[t, s], s_kv.at[i, t], r_z.at[z], 2 * pz + x, hb + t, start)
        kk = worker_of(s)
        for i in range(3):
            pz = 4 * c + i
            cols = pl.ds(i * HD, HD)
            put(q.at[:, cols], qb.at[s // 4], s_q.at[i], r_q.at[s // 4], 2 * pz + lax.rem(kk, 2), hb + kk // 2, start)
            for px in range(2):
                for pc in range(2):
                    put(meta, mt.at[s], s_m.at[i, px, pc], r_m, 2 * pz + px, hb + pc, start)

    all_sends(True)

    def source_at(n):
        far = (n + 1) // 2
        return lax.rem(z + jnp.where(lax.rem(n, 2) == 1, far, 8 - far), 8)

    def to_sibling(piece):
        return remote(kv.at[c, piece], kv.at[c, piece], s_f.at[0, piece], r_s.at[piece], s, hb + 1 - c)

    def to_partner(zs):
        piece = 2 * zs + x
        return remote(kv.at[c, piece], kv.at[c, piece], s_f.at[1, zs], r_x.at[zs], 2 * z + 1 - x, hb + c)

    @pl.when(lax.rem(z, 4) < 3)
    def _():
        def turn(n, _):
            @pl.when(n < 8)
            def _():
                zs = source_at(n)
                piece = 2 * zs + x
                pltpu.make_async_copy(kv.at[c, piece], kv.at[c, piece], r_z.at[zs]).wait()
                to_partner(zs).start()
                to_sibling(piece).start()

            @pl.when(n > 0)
            def _():
                zs = source_at(n - 1)
                piece = 2 * zs + 1 - x
                pltpu.make_async_copy(kv.at[c, piece], kv.at[c, piece], r_x.at[zs]).wait()
                to_sibling(piece).start()

            return 0

        lax.fori_loop(0, 9, turn, 0)
        for j in range(4):
            pltpu.make_async_copy(qb.at[j], qb.at[j], r_q.at[j]).wait()
        pltpu.make_async_copy(mt, mt, r_m).wait()

        def settle(n, _):
            pltpu.make_async_copy(kv.at[1 - c, n], kv.at[1 - c, n], r_s.at[n]).wait()
            to_sibling(n).wait_send()
            return 0

        lax.fori_loop(0, 16, settle, 0)

        def sent(n, _):
            to_partner(n).wait_send()
            return 0

        lax.fori_loop(0, 8, sent, 0)

    all_sends(False)


def spread(q, k, v, meta):
    dma = pltpu.SemaphoreType.DMA
    tok = q.shape[0]
    return pl.pallas_call(
        spread_kernel,
        name="spread",
        out_shape=(
            jax.ShapeDtypeStruct((4, tok, HD), q.dtype),
            jax.ShapeDtypeStruct((2, 16, tok, HD), q.dtype),
            jax.ShapeDtypeStruct((16, 1, 128), jnp.int32),
        ),
        in_specs=[pl.BlockSpec(memory_space=ANY)] * 4,
        out_specs=[pl.BlockSpec(memory_space=ANY)] * 3,
        scratch_shapes=[
            dma((3, 2)), dma((3,)), dma((3, 2, 2)), dma((2, 16)),
            dma((8,)), dma((8,)), dma((16,)), dma((4,)), dma,
        ],
        compiler_params=pltpu.CompilerParams(collective_id=0, has_side_effects=True),
    )(q, k, v, meta)


GROUP = 4


def attend_kernel(meta, q_ref, kv_ref, o_ref, table, vext, acc, peak):
    s, hb, c, z, x = where_am_i()
    kk = 2 * c + x
    factor = math.log2(math.e) / math.sqrt(HD)

    @pl.when(lax.rem(z, 4) < 3)
    def _():
        def widen(n, _):
            vext[n, :, :HD] = kv_ref[1, n]
            vext[n, :, HD:] = jnp.ones((2 * BLK, HD), jnp.bfloat16)
            return 0

        lax.fori_loop(0, 16, widen, 0)

        def one_block(b, _):
            j, half = b // 2, lax.rem(b, 2)
            owner = jnp.where(
                j == 0, kk, jnp.where(j == 1, 7 - kk, jnp.where(j == 2, 8 + kk, 15 - kk))
            )
            row = 2 * owner + half
            frame = meta[owner, 0, 64 + half]

            def scan(d, count):
                for e in range(2):
                    near = meta[owner, 0, half * 32 + 2 * d + e] == 1
                    same = meta[d, 0, 64 + e] == frame
                    ok = ((2 * d + e <= row) & near) | same
                    table[count] = 2 * d + e
                    count = count + ok.astype(jnp.int32)
                return count

            count = lax.fori_loop(0, jnp.minimum(16, owner + 3), scan, 0)
            rows = pl.ds(pl.multiple_of(half * BLK, BLK), BLK)
            q = q_ref[j, rows, :]
            acc[...] = jnp.zeros_like(acc)
            peak[...] = jnp.full_like(peak, -1e30)

            def step(first, many):
                scores = []
                values = []
                for u in range(many):
                    blk = table[first + u]
                    krows = pl.ds(pl.multiple_of(lax.rem(blk, 2) * BLK, BLK), BLK)
                    keys = kv_ref[0, blk // 2, krows, :]
                    values.append((blk // 2, krows))
                    scores.append(
                        lax.dot_general(q, keys, (((1,), (1,)), ((), ())), preferred_element_type=jnp.float32)
                    )
                top = scores[0]
                for more in scores[1:]:
                    top = jnp.maximum(top, more)
                old = peak[...]
                new = jnp.maximum(old, jnp.max(top, axis=1, keepdims=True))
                peak[...] = new
                shrink = jnp.exp2((old - new) * factor)
                added = None
                for u in range(many):
                    weight = jnp.exp2((scores[u] - new[:, :1]) * factor).astype(jnp.bfloat16)
                    part = jnp.dot(
                        weight, vext[values[u][0], values[u][1], :], preferred_element_type=jnp.float32
                    )
                    added = part if added is None else added + part
                acc[:, :HD] = acc[:, :HD] * shrink + added[:, :HD]
                acc[:, HD:] = acc[:, HD:] * shrink + added[:, HD:]

            whole = count // GROUP

            def group(g, _):
                step(g * GROUP, GROUP)
                return 0

            lax.fori_loop(0, whole, group, 0)

            def single(g, _):
                step(g, 1)
                return 0

            lax.fori_loop(whole * GROUP, count, single, 0)
            o_ref[j, rows, :] = (acc[:, :HD] / acc[:, HD:]).astype(jnp.bfloat16)
            return 0

        lax.fori_loop(0, 8, one_block, 0)


def attend(meta, q, kv):
    return pl.pallas_call(
        attend_kernel,
        name="attend",
        out_shape=jax.ShapeDtypeStruct(q.shape, q.dtype),
        in_specs=[
            pl.BlockSpec(memory_space=pltpu.SMEM),
            pl.BlockSpec(memory_space=pltpu.VMEM),
            pl.BlockSpec(memory_space=pltpu.VMEM),
        ],
        out_specs=pl.BlockSpec(memory_space=pltpu.VMEM),
        scratch_shapes=[
            pltpu.SMEM((36,), jnp.int32),
            pltpu.VMEM((16, 2 * BLK, 2 * HD), jnp.bfloat16),
            pltpu.VMEM((BLK, 2 * HD), jnp.float32),
            pltpu.VMEM((BLK, HD), jnp.float32),
        ],
        cost_estimate=pl.CostEstimate(flops=20_000_000_000, bytes_accessed=8_000_000, transcendentals=0),
    )(meta, q, kv)


def collect_kernel(o, attn, send, recv):
    s, hb, c, z, x = where_am_i()
    kk = 2 * c + x
    barrier = pltpu.get_barrier_semaphore()
    w = worker_of(s)
    for i in range(3):
        ps, ph = 2 * (4 * c + i) + lax.rem(w, 2), hb + w // 2

        @pl.when(jnp.logical_not((ps == s) & (ph == hb + c)))
        def _():
            pl.semaphore_signal(barrier, inc=1, device_id=(ps, ph), device_id_type=MESH)

    i = lax.rem(z, 4)
    to_head = hb + z // 4
    cols = pl.ds(pl.multiple_of(i * HD, HD), HD)

    def each(fn):
        for j in range(4):
            to = chunk_owner(kk, j)
            mine = (to == s) & (to_head == hb + c)
            fn(j, to, mine)

    @pl.when(i < 3)
    def _():
        own = sum(((chunk_owner(kk, j) == s) & (to_head == hb + c)).astype(jnp.int32) for j in range(4))
        pl.semaphore_wait(barrier, 4 - own)

        def begin(j, to, mine):
            @pl.when(mine)
            def _():
                pltpu.make_async_copy(o.at[j], attn.at[:, cols], recv.at[i]).start()

            @pl.when(jnp.logical_not(mine))
            def _():
                remote(o.at[j], attn.at[:, cols], send.at[j], recv.at[i], to, to_head).start()

        each(begin)

    for n in range(3):
        got = attn.at[:, pl.ds(n * HD, HD)]
        pltpu.make_async_copy(got, got, recv.at[n]).wait()

    @pl.when(i < 3)
    def _():
        def sent(j, to, mine):
            @pl.when(jnp.logical_not(mine))
            def _():
                remote(o.at[j], attn.at[:, cols], send.at[j], recv.at[i], to, to_head).wait_send()

        each(sent)


def collect(o):
    tok = o.shape[1]
    return pl.pallas_call(
        collect_kernel,
        name="collect",
        out_shape=jax.ShapeDtypeStruct((tok, 3 * HD), o.dtype),
        in_specs=[pl.BlockSpec(memory_space=ANY)],
        out_specs=pl.BlockSpec(memory_space=ANY),
        scratch_shapes=[pltpu.SemaphoreType.DMA((4,)), pltpu.SemaphoreType.DMA((3,))],
        compiler_params=pltpu.CompilerParams(collective_id=1, has_side_effects=True),
    )(o)


def body(queries, keys, values, frame_of_block, pair_mask, w_out):
    turned = lax.ppermute(
        w_out, ("seq", "head"), [(a * 16 + b, b * 16 + a) for a in range(16) for b in range(16)]
    )
    columns = lax.all_gather(turned, "seq", axis=0, tiled=True)
    meta = jnp.concatenate(
        [pair_mask.reshape(-1), frame_of_block, jnp.zeros((62,), jnp.int32)]
    ).reshape(1, 128)
    qb, kv, mt = spread(queries, keys, values, meta)
    o = attend(mt, qb, kv)
    attn = collect(o)
    full_attn = lax.all_gather(attn, "head", axis=1, tiled=True)
    return jnp.dot(full_attn, columns, preferred_element_type=jnp.float32).astype(jnp.bfloat16)


def solution(mesh):
    return jax.shard_map(
        body,
        mesh=mesh,
        in_specs=(
            P("seq", "head"),
            P("seq", "head"),
            P("seq", "head"),
            P("seq"),
            P("seq", None),
            P("head", "seq"),
        ),
        out_specs=P("seq", "head"),
        check_vma=False,
    )
```

time: 463 us -> 296 us (0.64)
  Pallas kernels: 0 us -> 163 us
  waiting for transfers between devices: 217 us -> 97.3 us
  blocking collectives: 91.8 us -> 0 us
  starting transfers between devices: 54.8 us -> 7.62 us
  matrix products: 52 us -> 8.31 us
  other arithmetic: 14.3 us -> 1.32 us
  local copies, waits for them, and re-layouts: 12.9 us -> 1.47 us
    ppermute x45 -> x1, waiting for transfers between devices: 200 us -> 19.8 us  [body(): lax.ppermute(w_out, ('seq', 'head'), [(a * 16 + b, b * 16 + a) for a in r...]
    pallas_call x0 -> x3, Pallas kernels: none -> 163 us  [the longest x1 99.9 us: spread(): pl.pallas_call(spread_kernel, name='spread', out_shape=(jax.ShapeDtypeStr...]
    all_to_all x1 -> x0, blocking collectives: 83.1 us -> none  [body(): lax.all_to_all(wide_rows, 'head', split_axis=1, concat_axis=0, tiled=True)]
    all_gather x1, waiting for transfers between devices: 16.9 us -> 77.5 us  [body(): full_attn = lax.all_gather(attn, 'head', axis=1, tiled=True)]
    ppermute x45 -> x1, starting transfers between devices: 54.7 us -> 7.58 us  [body(): lax.ppermute(w_out, ('seq', 'head'), [(a * 16 + b, b * 16 + a) for a in r...]
    dot_general x49 -> x1, matrix products: 52 us -> 8.31 us  [body(): jnp.dot(full_attn, columns, preferred_element_type=jnp.float32)]
    reduce_sum x16 -> x0, other arithmetic: 12.9 us -> none  [update(): new_total = total * factor + jnp.sum(weight, axis=2)]
    all_gather x1 -> x0, blocking collectives: 8.66 us -> none  [whole_of(): out = lax.all_gather(out, axes[number], axis=dim, tiled=True)]
  transfers between devices with their start and end apart: 47 -> 3, of which waited for: 31 -> 2; matrix products, arithmetic and copies ran while one was open for 15% -> 1% of each run, Pallas kernels for 0% -> 56%
where the time goes in v1:
time: 296 us; the launch traced here: 292 us
  Pallas kernels  163 us (55%)
  waiting for transfers between devices  97.3 us (33%)
  between operations  13.4 us (5%)
  matrix products  8.31 us (3%)
  starting transfers between devices  7.62 us (3%)
    pallas_call x1, Pallas kernels, spread(): pl.pallas_call(spread_kernel, name='spread', out_shape=(jax.ShapeDtypeStr...  99.9 us
    all_gather x1, waiting for transfers between devices, body(): full_attn = lax.all_gather(attn, 'head', axis=1, tiled=True)  77.5 us
    pallas_call x1, Pallas kernels, attend(): pl.pallas_call(attend_kernel, name='attend', out_shape=jax.ShapeDtypeStru...  35.2 us
    pallas_call x1, Pallas kernels, collect(): pl.pallas_call(collect_kernel, name='collect', out_shape=jax.ShapeDtypeSt...  27.7 us
    ppermute x1, waiting for transfers between devices, body(): lax.ppermute(w_out, ('seq', 'head'), [(a * 16 + b, b * 16 + a) for a in r...  19.8 us
    dot_general x1, matrix products, body(): jnp.dot(full_attn, columns, preferred_element_type=jnp.float32)  8.31 us
    ppermute x1, starting transfers between devices, body(): lax.ppermute(w_out, ('seq', 'head'), [(a * 16 + b, b * 16 + a) for a in r...  7.58 us
  transfers between devices with their start and end apart: 3, of which 2 were waited for; matrix products, arithmetic and copies ran while one was open for 1% of the time, Pallas kernels for 56%

profile of v1, /device:TPU:27, one launch (start us, length us, event | category | flops | bytes accessed | tf_op | source)
XLA Modules:
  0.0 292.3 jit_solution(12875543417165769388)
XLA Ops:
  6.5 0.0 all-gather.5.cloned.1.call-start
  6.5 7.6 %collective-permute-start = (bf16[384,384]{1,0:T(8,128)(2,1)}, bf16[384,384]{1,0:T(8,128)(2,1)S(1)}, u32[]{:S(2)}, u32[]{:S(2)}) collective-permute-start(bf16[384,384]{1,0:T(8,128)(2,1)} %param.11), channel_id=1, source_target_pairs={{0,0},{1,16},{2,32},{3,48},{4,64},{5,80},{6,96},{7,112},{8,128},{9... | collective-permute-start | bytes 884744 | tf_op jit(solution)/shard_map/ppermute | solution.py:336
  14.1 19.8 %collective-permute-done = bf16[384,384]{1,0:T(8,128)(2,1)S(1)} collective-permute-done((bf16[384,384]{1,0:T(8,128)(2,1)}, bf16[384,384]{1,0:T(8,128)(2,1)S(1)}, u32[]{:S(2)}, u32[]{:S(2)}) %collective-permute-start) | collective-permute-done | bytes 294944 | tf_op jit(solution)/shard_map/ppermute | solution.py:336
  33.9 0.0 copy-start
  33.9 0.7 copy-done
  34.6 0.0 all-gather.5.cloned.1.call-update
  34.6 0.0 all-gather.3.cloned.1.call-start
  34.7 0.8 reshape.6
  35.4 1.3 add_bitcast_fusion.meta
  36.8 99.9 %spread.1 = (bf16[4,512,128]{2,1,0:T(8,128)(2,1)}, bf16[2,16,512,128]{3,2,1,0:T(8,128)(2,1)}, s32[16,1,128]{2,1,0:T(1,128)}) custom-call(bf16[512,384]{1,0:T(8,128)(2,1)} %q.1, bf16[512,384]{1,0:T(8,128)(2,1)} %k.1, bf16[512,384]{1,0:T(8,128)(2,1)} %v.1, s32[1,128]{1,0:T(1,128)} %add_bitcast_fusion.meta), custom_call_target="tpu_custom_call" | custom-call | tf_op jit(solution)/shard_map/spread/pallas_call | solution.py:144
  136.7 35.2 %attend.1.o = bf16[4,512,128]{2,1,0:T(8,128)(2,1)} custom-call(s32[16,1,128]{2,1,0:T(1,128)} %get-tuple-element.8.meta, bf16[4,512,128]{2,1,0:T(8,128)(2,1)} %get-tuple-element.9.q_ref, bf16[2,16,512,128]{3,2,1,0:T(8,128)(2,1)} %get-tuple-element.10.kv_ref), custom_call_target="tpu_custom_call" | custom-call | flops 20000000000 | bytes 8000000 | tf_op jit(solution)/shard_map/attend/pallas_call | solution.py:250
  171.9 27.7 %collect.1 = bf16[512,384]{1,0:T(8,128)(2,1)} custom-call(bf16[4,512,128]{2,1,0:T(8,128)(2,1)} %attend.1.o), custom_call_target="tpu_custom_call" | custom-call | tf_op jit(solution)/shard_map/collect/pallas_call | solution.py:324
  199.6 0.0 all-gather.3.cloned.1.call-update
  199.6 0.0 all-gather.5.cloned.1.call-done
  199.6 77.5 %all-gather.3.cloned.1.call-done = bf16[512,6144]{1,0:T(8,128)(2,1)} async-done(((bf16[512,384]{1,0:T(8,128)(2,1)}), bf16[512,6144]{1,0:T(8,128)(2,1)}) %all-gather.3.cloned.1.call-update) | async-done | bytes 6291472 | tf_op jit(solution)/shard_map/all_gather | solution.py:346
  277.1 8.3 %convolution_convert_fusion = bf16[512,384]{1,0:T(8,128)(2,1)} fusion(bf16[512,6144]{1,0:T(8,128)(2,1)} %all-gather.3.cloned.1.call-done, bf16[6144,384]{1,0:T(8,128)(2,1)} %all-gather.5.cloned.1.call-done), kind=kOutput, calls=%fused_computation | convolution fusion | flops 2416115712 | bytes 11403264 | tf_op jit(solution)/shard_map/dot_general | solution.py:347
  (1 shorter events, 0.0 us)
Async XLA Ops:
  6.5 193.1 %all-gather.5.cloned.1.call-start = ((), (), s32[]{:S(2)}) async-start(), calls=%async_computation.1 | async-start | bytes 5013504 | tf_op jit(solution)/shard_map/all_gather | solution.py:339
  6.5 27.4 %collective-permute-start = (bf16[384,384]{1,0:T(8,128)(2,1)}, bf16[384,384]{1,0:T(8,128)(2,1)S(1)}, u32[]{:S(2)}, u32[]{:S(2)}) collective-permute-start(bf16[384,384]{1,0:T(8,128)(2,1)} %param.11), channel_id=1, source_target_pairs={{0,0},{1,16},{2,32},{3,48},{4,64},{5,80},{6,96},{7,112},{8,128},{9... | collective-permute-start | bytes 884744 | tf_op jit(solution)/shard_map/ppermute | solution.py:336
  33.9 0.7 copy-start
  34.6 242.5 %all-gather.3.cloned.1.call-start = ((), (), s32[]{:S(2)}) async-start(), calls=%async_computation | async-start | bytes 6684672 | tf_op jit(solution)/shard_map/all_gather | solution.py:346
Sparse Core Ops, SparseCore 0:
  34.8 145.3 all-gather.4
  199.7 77.3 all-gather.2

commit v2 on v1

--- a/solution.py
+++ b/solution.py
@@ -35,8 +35,9 @@
     )
 
 
-def spread_kernel(q, k, v, meta, qb, kv, mt, s_kv, s_q, s_m, s_f, r_z, r_x, r_s, r_q, r_m):
+def spread_kernel(q, k, v, meta, w, qb, kv, mt, wb, s_kv, s_q, s_m, s_f, s_w, r_z, r_x, r_s, r_q, r_m, r_w):
     s, hb, c, z, x = where_am_i()
+    y, x_hi = hb // 4, lax.rem(hb, 4) // 2
     barrier = pltpu.get_barrier_semaphore()
 
     def greet(n, _):
@@ -49,7 +50,14 @@
         return 0
 
     lax.fori_loop(0, 32, greet, 0)
-    pl.semaphore_wait(barrier, 31)
+
+    def greet_row(n, _):
+        other = 4 * y + 2 * (1 - x_hi) + n
+        pl.semaphore_signal(barrier, inc=1, device_id=(s, other), device_id_type=MESH)
+        return 0
+
+    lax.fori_loop(0, 2, greet_row, 0)
+    pl.semaphore_wait(barrier, 33)
 
     def put(src, dst, send, recv, seq, head, start):
         mine = (seq == s) & (head == hb + c)
@@ -70,6 +78,11 @@
                 copy.wait_send()
 
     def all_sends(start):
+        here = wb.at[lax.rem(z, 4) // 2, 2 * x_hi + c]
+        put(
+            w, here, s_w.at[2, 0, 0], r_w.at[lax.rem(z, 4) // 2, 2 * x_hi + c],
+            s, 4 * y + 2 * lax.rem(z, 2) + z // 4, start,
+        )
         for i in range(3):
             pz = 4 * c + i
             cols = pl.ds(i * HD, HD)
@@ -97,9 +110,50 @@
         piece = 2 * zs + x
         return remote(kv.at[c, piece], kv.at[c, piece], s_f.at[1, zs], r_x.at[zs], 2 * z + 1 - x, hb + c)
 
-    @pl.when(lax.rem(z, 4) < 3)
-    def _():
-        def turn(n, _):
+    def w_hop(e, r, up):
+        piece = wb.at[e, r]
+        to = lax.rem(z + (1 if up else 7), 8)
+        return remote(piece, piece, s_w.at[1 if up else 0, e, r], r_w.at[e, r], 2 * to + x, hb + c)
+
+    def w_far(e):
+        return lax.rem(z - (4 * c + 2 * e + x_hi) + 8, 8)
+
+    def w_turn(n):
+        for e in range(2):
+            far = w_far(e)
+            r = n - jnp.where(far > 4, 8 - far, far)
+
+            @pl.when((r >= 0) & (r < 4))
+            def _():
+                pltpu.make_async_copy(wb.at[e, r], wb.at[e, r], r_w.at[e, r]).wait()
+
+                @pl.when(far < 4)
+                def _():
+                    w_hop(e, r, True).start()
+
+                @pl.when((far == 0) | (far > 5))
+                def _():
+                    w_hop(e, r, False).start()
+
+    def w_sent(r, _):
+        for e in range(2):
+            far = w_far(e)
+
+            @pl.when(far < 4)
+            def _():
+                w_hop(e, r, True).wait_send()
+
+            @pl.when((far == 0) | (far > 5))
+            def _():
+                w_hop(e, r, False).wait_send()
+
+        return 0
+
+    working = lax.rem(z, 4) < 3
+
+    def turn(n, _):
+        @pl.when(working)
+        def _():
             @pl.when(n < 8)
             def _():
                 zs = source_at(n)
@@ -115,9 +169,13 @@
                 pltpu.make_async_copy(kv.at[c, piece], kv.at[c, piece], r_x.at[zs]).wait()
                 to_sibling(piece).start()
 
-            return 0
-
-        lax.fori_loop(0, 9, turn, 0)
+        w_turn(n)
+        return 0
+
+    lax.fori_loop(0, 9, turn, 0)
+
+    @pl.when(working)
+    def _():
         for j in range(4):
             pltpu.make_async_copy(qb.at[j], qb.at[j], r_q.at[j]).wait()
         pltpu.make_async_copy(mt, mt, r_m).wait()
@@ -135,10 +193,11 @@
 
         lax.fori_loop(0, 8, sent, 0)
 
+    lax.fori_loop(0, 4, w_sent, 0)
     all_sends(False)
 
 
-def spread(q, k, v, meta):
+def spread(q, k, v, meta, w):
     dma = pltpu.SemaphoreType.DMA
     tok = q.shape[0]
     return pl.pallas_call(
@@ -148,15 +207,16 @@
             jax.ShapeDtypeStruct((4, tok, HD), q.dtype),
             jax.ShapeDtypeStruct((2, 16, tok, HD), q.dtype),
             jax.ShapeDtypeStruct((16, 1, 128), jnp.int32),
+            jax.ShapeDtypeStruct((2, 4) + w.shape, w.dtype),
         ),
-        in_specs=[pl.BlockSpec(memory_space=ANY)] * 4,
-        out_specs=[pl.BlockSpec(memory_space=ANY)] * 3,
+        in_specs=[pl.BlockSpec(memory_space=ANY)] * 5,
+        out_specs=[pl.BlockSpec(memory_space=ANY)] * 4,
         scratch_shapes=[
-            dma((3, 2)), dma((3,)), dma((3, 2, 2)), dma((2, 16)),
-            dma((8,)), dma((8,)), dma((16,)), dma((4,)), dma,
+            dma((3, 2)), dma((3,)), dma((3, 2, 2)), dma((2, 16)), dma((3, 2, 4)),
+            dma((8,)), dma((8,)), dma((16,)), dma((4,)), dma, dma((2, 4)),
         ],
         compiler_params=pltpu.CompilerParams(collective_id=0, has_side_effects=True),
-    )(q, k, v, meta)
+    )(q, k, v, meta, w)
 
 
 GROUP = 4
@@ -267,84 +327,168 @@
     )(meta, q, kv)
 
 
-def collect_kernel(o, attn, send, recv):
-    s, hb, c, z, x = where_am_i()
-    kk = 2 * c + x
+def project_kernel(o, w, out, a, part, got, s_o, s_x, s_s, s_p, r_o, r_x, r_s, r_p):
+    s, hb, c, z, x_lo = where_am_i()
+    y, x_hi = hb // 4, lax.rem(hb, 4) // 2
+    x = 2 * x_hi + x_lo
+    kk = 2 * c + x_lo
     barrier = pltpu.get_barrier_semaphore()
-    w = worker_of(s)
+
+    def greet(seq, head):
+        pl.semaphore_signal(barrier, inc=1, device_id=(seq, head), device_id_type=MESH)
+
+    def greet_group(n, _):
+        ps, pc = n // 2, lax.rem(n, 2)
+
+        @pl.when(jnp.logical_not((ps == s) & (pc == c)))
+        def _():
+            greet(ps, hb + pc)
+
+        return 0
+
+    def greet_row(n, _):
+        greet(2 * z + n // 2, 4 * y + 2 * (1 - x_hi) + lax.rem(n, 2))
+        return 0
+
+    def greet_line(n, _):
+        py = lax.rem(y + 1 + n // 4, 4)
+        greet(2 * z + lax.rem(n, 4) // 2, 4 * py + 2 * x_hi + lax.rem(n, 2))
+        return 0
+
+    lax.fori_loop(0, 32, greet_group, 0)
+    lax.fori_loop(0, 4, greet_row, 0)
+    lax.fori_loop(0, 12, greet_line, 0)
+    pl.semaphore_wait(barrier, 47)
+
+    def move(src, dst, send, recv, seq, head, start):
+        mine = (seq == s) & (head == hb + c)
+        copy = remote(src, dst, send, recv, seq, head)
+        if start:
+
+            @pl.when(mine)
+            def _():
+                pltpu.make_async_copy(src, dst, recv).start()
+
+            @pl.when(jnp.logical_not(mine))
+            def _():
+                copy.start()
+        else:
+
+            @pl.when(jnp.logical_not(mine))
+            def _():
+                copy.wait_send()
+
+    def arrived(ref, sem):
+        pltpu.make_async_copy(ref, ref, sem).wait()
+
+    def cols(i):
+        return pl.ds(i * HD, HD)
+
+    third = lax.rem(z, 4)
+
+    def give_back(start):
+        @pl.when(third < 3)
+        def _():
+            lanes = pl.ds(pl.multiple_of(third * HD, HD), HD)
+            for j in range(4):
+                to = chunk_owner(kk, j)
+                slot = 2 * x_hi + lax.rem(to, 2)
+                move(o.at[j], a.at[slot, z // 4, :, lanes], s_o.at[j], r_o.at[third], to, hb + z // 4, start)
+
+    def to_sibling(slot, i):
+        piece = a.at[slot, c, :, cols(i)]
+        return remote(piece, piece, s_s.at[slot, i], r_s.at[slot, i], s, hb + 1 - c)
+
+    def to_row(dx, i):
+        px = lax.rem(x + dx, 4)
+        piece = a.at[x, c, :, cols(i)]
+        return remote(piece, piece, s_x.at[dx, i], r_x.at[x, i], 2 * z + lax.rem(px, 2), 4 * y + 2 * (px // 2) + c)
+
+    give_back(True)
     for i in range(3):
-        ps, ph = 2 * (4 * c + i) + lax.rem(w, 2), hb + w // 2
-
-        @pl.when(jnp.logical_not((ps == s) & (ph == hb + c)))
-        def _():
-            pl.semaphore_signal(barrier, inc=1, device_id=(ps, ph), device_id_type=MESH)
-
-    i = lax.rem(z, 4)
-    to_head = hb + z // 4
-    cols = pl.ds(pl.multiple_of(i * HD, HD), HD)
-
-    def each(fn):
-        for j in range(4):
-            to = chunk_owner(kk, j)
-            mine = (to == s) & (to_head == hb + c)
-            fn(j, to, mine)
-
-    @pl.when(i < 3)
-    def _():
-        own = sum(((chunk_owner(kk, j) == s) & (to_head == hb + c)).astype(jnp.int32) for j in range(4))
-        pl.semaphore_wait(barrier, 4 - own)
-
-        def begin(j, to, mine):
-            @pl.when(mine)
-            def _():
-                pltpu.make_async_copy(o.at[j], attn.at[:, cols], recv.at[i]).start()
-
-            @pl.when(jnp.logical_not(mine))
-            def _():
-                remote(o.at[j], attn.at[:, cols], send.at[j], recv.at[i], to, to_head).start()
-
-        each(begin)
-
-    for n in range(3):
-        got = attn.at[:, pl.ds(n * HD, HD)]
-        pltpu.make_async_copy(got, got, recv.at[n]).wait()
-
-    @pl.when(i < 3)
-    def _():
-        def sent(j, to, mine):
-            @pl.when(jnp.logical_not(mine))
-            def _():
-                remote(o.at[j], attn.at[:, cols], send.at[j], recv.at[i], to, to_head).wait_send()
-
-        each(sent)
-
-
-def collect(o):
+        arrived(a.at[x, c, :, cols(i)], r_o.at[i])
+        for dx in (1, 3, 2):
+            to_row(dx, i).start()
+        to_sibling(x, i).start()
+    for i in range(3):
+        for dx in (3, 1, 2):
+            slot = lax.rem(x + dx, 4)
+            arrived(a.at[slot, c, :, cols(i)], r_x.at[slot, i])
+            to_sibling(slot, i).start()
+    for slot in range(4):
+        for i in range(3):
+            arrived(a.at[slot, 1 - c, :, cols(i)], r_s.at[slot, i])
+
+    def pass_on(t, e, start):
+        py = 2 * c + e
+        move(part.at[t, e], got.at[y], s_p.at[t, e], r_p.at[y], 2 * z + t, 4 * py + 2 * x_hi + x_lo, start)
+
+    for t in range(2):
+        for e in range(2):
+
+            def tile(n, _):
+                rows = pl.ds(pl.multiple_of(n * 128, 128), 128)
+                total = None
+                for r in range(4):
+                    dot = jnp.dot(
+                        a[2 * (r // 2) + t, r % 2, rows, :], w[e, r], preferred_element_type=jnp.float32
+                    )
+                    total = dot if total is None else total + dot
+                part[t, e, rows, :] = total.astype(jnp.bfloat16)
+                return 0
+
+            lax.fori_loop(0, 4, tile, 0)
+            pass_on(t, e, True)
+    for n in range(4):
+        arrived(got.at[n], r_p.at[n])
+
+    def add(n, _):
+        rows = pl.ds(pl.multiple_of(n * 64, 64), 64)
+        total = got[0, rows, :].astype(jnp.float32)
+        for m in range(1, 4):
+            total = total + got[m, rows, :].astype(jnp.float32)
+        out[rows, :] = total.astype(jnp.bfloat16)
+        return 0
+
+    lax.fori_loop(0, 8, add, 0)
+    give_back(False)
+    for i in range(3):
+        for dx in (1, 2, 3):
+            to_row(dx, i).wait_send()
+        for slot in range(4):
+            to_sibling(slot, i).wait_send()
+    for t in range(2):
+        for e in range(2):
+            pass_on(t, e, False)
+
+
+def project(o, w):
+    dma = pltpu.SemaphoreType.DMA
     tok = o.shape[1]
+    wide = 3 * HD
     return pl.pallas_call(
-        collect_kernel,
-        name="collect",
-        out_shape=jax.ShapeDtypeStruct((tok, 3 * HD), o.dtype),
-        in_specs=[pl.BlockSpec(memory_space=ANY)],
-        out_specs=pl.BlockSpec(memory_space=ANY),
-        scratch_shapes=[pltpu.SemaphoreType.DMA((4,)), pltpu.SemaphoreType.DMA((3,))],
+        project_kernel,
+        name="project",
+        out_shape=jax.ShapeDtypeStruct((tok, wide), o.dtype),
+        in_specs=[pl.BlockSpec(memory_space=pltpu.VMEM)] * 2,
+        out_specs=pl.BlockSpec(memory_space=pltpu.VMEM),
+        scratch_shapes=[
+            pltpu.VMEM((4, 2, tok, wide), jnp.bfloat16),
+            pltpu.VMEM((2, 2, tok, wide), jnp.bfloat16),
+            pltpu.VMEM((4, tok, wide), jnp.bfloat16),
+            dma((4,)), dma((4, 3)), dma((4, 3)), dma((2, 2)),
+            dma((3,)), dma((4, 3)), dma((4, 3)), dma((4,)),
+        ],
         compiler_params=pltpu.CompilerParams(collective_id=1, has_side_effects=True),
-    )(o)
+    )(o, w)
 
 
 def body(queries, keys, values, frame_of_block, pair_mask, w_out):
-    turned = lax.ppermute(
-        w_out, ("seq", "head"), [(a * 16 + b, b * 16 + a) for a in range(16) for b in range(16)]
-    )
-    columns = lax.all_gather(turned, "seq", axis=0, tiled=True)
     meta = jnp.concatenate(
         [pair_mask.reshape(-1), frame_of_block, jnp.zeros((62,), jnp.int32)]
     ).reshape(1, 128)
-    qb, kv, mt = spread(queries, keys, values, meta)
-    o = attend(mt, qb, kv)
-    attn = collect(o)
-    full_attn = lax.all_gather(attn, "head", axis=1, tiled=True)
-    return jnp.dot(full_attn, columns, preferred_element_type=jnp.float32).astype(jnp.bfloat16)
+    qb, kv, mt, wb = spread(queries, keys, values, meta, w_out)
+    return project(attend(mt, qb, kv), wb)
 
 
 def solution(mesh):

time: 296 us -> 189 us (0.64)
  the two profiles are of different devices: /device:TPU:27 before, /device:TPU:75 now
where the time goes in v2:
time: 189 us
  Pallas kernels  185 us (98%)
  local copies, waits for them, and re-layouts  2.54 us (1%)
    pallas_call x1, Pallas kernels, spread(): pl.pallas_call(spread_kernel, name='spread', out_shape=(jax.ShapeDtypeStr...  75.3 us
    pallas_call x1, Pallas kernels, project(): pl.pallas_call(project_kernel, name='project', out_shape=jax.ShapeDtypeSt...  71.7 us
    pallas_call x1, Pallas kernels, attend(): pl.pallas_call(attend_kernel, name='attend', out_shape=jax.ShapeDtypeStru...  37.8 us

profile of v2, /device:TPU:75, one launch (start us, length us, event | category | flops | bytes accessed | tf_op | source)
XLA Modules:
  0.0 188.6 jit_solution(2288947366644001755)
XLA Ops:
  0.0 0.8 reshape.6
  0.8 1.2 add_bitcast_fusion.meta
  2.0 75.3 %spread.1 = (bf16[4,512,128]{2,1,0:T(8,128)(2,1)}, bf16[2,16,512,128]{3,2,1,0:T(8,128)(2,1)}, s32[16,1,128]{2,1,0:T(1,128)}, bf16[2,4,384,384]{3,2,1,0:T(8,128)(2,1)}) custom-call(bf16[512,384]{1,0:T(8,128)(2,1)} %q.1, bf16[512,384]{1,0:T(8,128)(2,1)} %k.1, bf16[512,384]{1,0:T(8,128)(2,1)} %v.1, s32[1,128]{1,0:T(1,128)} %add_bitcast_fusion.meta, ...), custom_call_target="tpu_custom_call" | custom-call | tf_op jit(solution)/shard_map/spread/pallas_call | solution.py:203
  77.3 37.8 %attend.1.o = bf16[4,512,128]{2,1,0:T(8,128)(2,1)} custom-call(s32[16,1,128]{2,1,0:T(1,128)} %get-tuple-element.9.meta, bf16[4,512,128]{2,1,0:T(8,128)(2,1)} %get-tuple-element.10.q_ref, bf16[2,16,512,128]{3,2,1,0:T(8,128)(2,1)} %get-tuple-element.11.kv_ref), custom_call_target="tpu_custom_call" | custom-call | flops 20000000000 | bytes 8000000 | tf_op jit(solution)/shard_map/attend/pallas_call | solution.py:310
  115.1 71.7 %project.1 = bf16[512,384]{1,0:T(8,128)(2,1)} custom-call(bf16[4,512,128]{2,1,0:T(8,128)(2,1)} %attend.1.o, bf16[2,4,384,384]{3,2,1,0:T(8,128)(2,1)} %get-tuple-element.12.w), custom_call_target="tpu_custom_call" | custom-call | tf_op jit(solution)/shard_map/project/pallas_call | solution.py:469
  186.9 1.8 copy.8
  (1 shorter events, 0.0 us)

commit v3 on v0

v3 whole, which is shorter than its diff:
```python
import math

import jax
import jax.numpy as jnp
from jax import lax
from jax.experimental import pallas as pl
from jax.experimental.pallas import tpu as pltpu
from jax.sharding import PartitionSpec as P

HD = 128
BLK = 256
TOK = 512
MESH = pl.DeviceIdType.MESH
VMEM = pltpu.VMEM
FACTOR = math.log2(math.e) / math.sqrt(HD)


def remote(src, dst, send, recv, seq, head):
    return pltpu.make_async_remote_copy(
        src_ref=src, dst_ref=dst, send_sem=send, recv_sem=recv, device_id=(seq, head), device_id_type=MESH
    )


def arrived(ref, sem):
    pltpu.make_async_copy(ref, ref, sem).wait()


def chunk_owner(kk, j):
    return jnp.where(j == 0, kk, jnp.where(j == 1, 7 - kk, jnp.where(j == 2, 8 + kk, 15 - kk)))


def kernel(
    q, k, v, meta, w, out,
    qb, kv, mt, table, wb, acc, peak, ob, a, part, got,
    s_q, s_kv, s_m, s_f, s_p, s_w, r_q, r_z, r_x, r_s, r_m, r_w, r_t,
    s_o, s_a, s_b, s_d, r_o, r_a, r_b, r_d,
):
    s, h = lax.axis_index("seq"), lax.axis_index("head")
    c = lax.rem(h, 2)
    hb = h - c
    z, x_lo = s // 2, lax.rem(s, 2)
    y, x_hi = hb // 4, lax.rem(hb, 4) // 2
    x = 2 * x_hi + x_lo
    kk = 2 * c + x_lo
    third = lax.rem(z, 4)
    working = third < 3
    barrier = pltpu.get_barrier_semaphore()

    def greet(seq, head):
        pl.semaphore_signal(barrier, inc=1, device_id=(seq, head), device_id_type=MESH)

    def greet_group(n, _):
        ps, pc = n // 2, lax.rem(n, 2)

        @pl.when(jnp.logical_not((ps == s) & (pc == c)))
        def _():
            greet(ps, hb + pc)

        return 0

    def greet_row(n, _):
        greet(2 * z + n // 2, 4 * y + 2 * (1 - x_hi) + lax.rem(n, 2))
        return 0

    def greet_line(n, _):
        py = lax.rem(y + 1 + n // 4, 4)
        greet(2 * z + lax.rem(n, 4) // 2, 4 * py + 2 * x_hi + lax.rem(n, 2))
        return 0

    lax.fori_loop(0, 32, greet_group, 0)
    lax.fori_loop(0, 4, greet_row, 0)
    lax.fori_loop(0, 12, greet_line, 0)
    pl.semaphore_wait(barrier, 47)

    def put(src, dst, send, recv, seq, head, start):
        mine = (seq == s) & (head == h)
        copy = remote(src, dst, send, recv, seq, head)
        if start:

            @pl.when(mine)
            def _():
                pltpu.make_async_copy(src, dst, recv).start()

            @pl.when(jnp.logical_not(mine))
            def _():
                copy.start()
        else:

            @pl.when(jnp.logical_not(mine))
            def _():
                copy.wait_send()

    def cols(i):
        return pl.ds(i * HD, HD)

    rising = lax.rem(z - 4 * c + 9, 8) < 2
    low = lax.rem(s, 8)
    worker = jnp.where(low < 4, low, 7 - low)

    def spread(start):
        for r in range(3):
            i = jnp.where(rising | (z == 4 * c + 6 - 8 * c), r, 2 - r)
            pz = 4 * c + i
            lanes = pl.ds(pl.multiple_of(i * HD, HD), HD)
            put(q.at[:, lanes], qb.at[s // 4], s_q.at[r], r_q.at[s // 4], 2 * pz + lax.rem(worker, 2), hb + worker // 2, start)
        for r in range(3):
            i = jnp.where(rising | (z == 4 * c + 6 - 8 * c), r, 2 - r)
            pz = 4 * c + i
            lanes = pl.ds(pl.multiple_of(i * HD, HD), HD)
            for px in range(2):
                for pc in range(2):
                    put(meta, mt.at[s], s_m.at[r, px, pc], r_m, 2 * pz + px, hb + pc, start)
            for t, src in ((0, k), (1, v)):
                put(src.at[:, lanes], kv.at[t, s], s_kv.at[r, t], r_z.at[z], 2 * pz + x_lo, hb + t, start)
        e, r = lax.rem(z, 4) // 2, 2 * x_hi + c
        put(w, wb.at[e, r], s_w.at[2, 0, 0], r_w.at[e, r], s, 4 * y + 2 * lax.rem(z, 2) + z // 4, start)

    spread(True)

    def source_at(n):
        far = (n + 1) // 2
        return lax.rem(z + jnp.where(lax.rem(n, 2) == 1, far, 8 - far), 8)

    def to_sibling(piece):
        return remote(kv.at[c, piece], kv.at[c, piece], s_f.at[piece], r_s.at[piece], s, hb + 1 - c)

    def to_partner(zs):
        piece = 2 * zs + x_lo
        return remote(kv.at[c, piece], kv.at[c, piece], s_p.at[zs], r_x.at[zs], 2 * z + 1 - x_lo, h)

    def w_hop(e, r, up):
        to = lax.rem(z + (1 if up else 7), 8)
        return remote(wb.at[e, r], wb.at[e, r], s_w.at[1 if up else 0, e, r], r_w.at[e, r], 2 * to + x_lo, h)

    def w_far(e):
        return lax.rem(z - (4 * c + 2 * e + x_hi) + 8, 8)

    def w_turn(n):
        for e in range(2):
            far = w_far(e)
            r = n - jnp.where(far > 4, 8 - far, far)

            @pl.when((r >= 0) & (r < 4))
            def _():
                arrived(wb.at[e, r], r_w.at[e, r])

                @pl.when(far < 4)
                def _():
                    w_hop(e, r, True).start()

                @pl.when((far == 0) | (far > 5))
                def _():
                    w_hop(e, r, False).start()

    def w_sent(r, _):
        for e in range(2):
            far = w_far(e)

            @pl.when(far < 4)
            def _():
                w_hop(e, r, True).wait_send()

            @pl.when((far == 0) | (far > 5))
            def _():
                w_hop(e, r, False).wait_send()

        return 0

    def attend(piece, j, owner):
        keys = [kv[0, piece, pl.ds(u * BLK, BLK), :] for u in range(2)]
        ones = jnp.ones((BLK, HD), jnp.bfloat16)
        wide = [jnp.concatenate([kv[1, piece, pl.ds(u * BLK, BLK), :], ones], axis=1) for u in range(2)]
        for tile in range(4):
            half = tile // 2
            ok = []
            for u in range(2):
                near = (table[owner, 0, 32 * half + 2 * piece + u] == 1) & (2 * piece + u <= 2 * owner + half)
                ok.append(near | (table[piece, 0, 64 + u] == table[owner, 0, 64 + half]))
            rows = pl.ds(tile * 128, 128)
            held = pl.ds(pl.multiple_of(j * TOK + tile * 128, 128), 128)
            query = qb[j, rows, :]
            score = [
                lax.dot_general(query, keys[u], (((1,), (1,)), ((), ())), preferred_element_type=jnp.float32)
                for u in range(2)
            ]
            tops = [
                jnp.maximum(score[u][:, :HD], score[u][:, HD:]) + jnp.where(ok[u], 0.0, -1e30) for u in range(2)
            ]
            old = peak[held, :]
            new = jnp.maximum(old, jnp.max(jnp.maximum(tops[0], tops[1]), axis=1, keepdims=True))
            peak[held, :] = new
            shrink = jnp.exp2((old - new) * FACTOR)
            added = None
            for u in range(2):
                base = jnp.where(ok[u], new, 1e30)
                weight = jnp.concatenate(
                    [
                        jnp.exp2((score[u][:, cols_] - base) * FACTOR).astype(jnp.bfloat16)
                        for cols_ in (slice(0, HD), slice(HD, 2 * HD))
                    ],
                    axis=1,
                )
                dot = jnp.dot(weight, wide[u], preferred_element_type=jnp.float32)
                added = dot if added is None else added + dot
            acc[held, :HD] = acc[held, :HD] * shrink + added[:, :HD]
            acc[held, HD:] = acc[held, HD:] * shrink + added[:, HD:]

    @pl.when(working)
    def _():
        acc[...] = jnp.zeros_like(acc)
        peak[...] = jnp.full_like(peak, -1e30)

    def turn(n, _):
        @pl.when(working & (n < 8))
        def _():
            zs = source_at(n)
            piece = 2 * zs + x_lo
            arrived(kv.at[c, piece], r_z.at[zs])
            to_partner(zs).start()
            to_sibling(piece).start()

        @pl.when(working & (n > 0) & (n < 9))
        def _():
            zs = source_at(n - 1)
            piece = 2 * zs + 1 - x_lo
            arrived(kv.at[c, piece], r_x.at[zs])
            to_sibling(piece).start()

        @pl.when(n >= W_LAG)
        def _():
            w_turn(n - W_LAG)

        @pl.when(working & (n == 2))
        def _():
            for j in range(4):
                arrived(qb.at[j], r_q.at[j])
            arrived(mt, r_m)
            local = pltpu.make_async_copy(mt, table, r_t)
            local.start()
            local.wait()

        @pl.when(working & (n > 1) & (n < 10))
        def _():
            zs = source_at(n - 2)
            for side in range(2):
                piece = 2 * zs + side
                arrived(kv.at[1 - c, piece], r_s.at[piece])

            def one(m, _):
                piece, j = 2 * zs + m // 4, lax.rem(m, 4)
                owner = chunk_owner(kk, j)

                @pl.when(piece <= owner + 2)
                def _():
                    attend(piece, j, owner)

                return 0

            lax.fori_loop(0, 8, one, 0)

        return 0

    lax.fori_loop(0, max(10, 8 + W_LAG), turn, 0)

    def give_back(start):
        lanes = pl.ds(pl.multiple_of(third * HD, HD), HD)
        for j in range(4):
            to = chunk_owner(kk, j)
            slot = 2 * x_hi + lax.rem(to, 2)
            put(ob.at[j], a.at[slot, z // 4, :, lanes], s_o.at[j], r_o.at[third], to, hb + z // 4, start)

    @pl.when(working)
    def _():
        def finish(n, _):
            rows = pl.ds(pl.multiple_of(n * 128, 128), 128)
            ob[n // 4, pl.ds(pl.multiple_of(lax.rem(n, 4) * 128, 128), 128), :] = (
                acc[rows, :HD] / acc[rows, HD:]
            ).astype(jnp.bfloat16)
            return 0

        lax.fori_loop(0, 16, finish, 0)
        give_back(True)

    def cross(slot, i):
        piece = a.at[slot, c, :, cols(i)]
        return remote(piece, piece, s_b.at[slot, i], r_b.at[slot, i], s, hb + 1 - c)

    def to_row(dx, i):
        px = lax.rem(x + dx, 4)
        piece = a.at[x, c, :, cols(i)]
        return remote(piece, piece, s_a.at[dx, i], r_a.at[x, i], 2 * z + lax.rem(px, 2), 4 * y + 2 * (px // 2) + c)

    for i in range(3):
        arrived(a.at[x, c, :, cols(i)], r_o.at[i])
        for dx in (1, 3, 2):
            to_row(dx, i).start()
        cross(x, i).start()
    for i in range(3):
        for dx in (3, 1, 2):
            slot = lax.rem(x + dx, 4)
            arrived(a.at[slot, c, :, cols(i)], r_a.at[slot, i])
            cross(slot, i).start()
    for slot in range(4):
        for i in range(3):
            arrived(a.at[slot, 1 - c, :, cols(i)], r_b.at[slot, i])

    def pass_on(t, e, start):
        py = 2 * c + e
        put(part.at[t, e], got.at[y], s_d.at[t, e], r_d.at[y], 2 * z + t, 4 * py + 2 * x_hi + x_lo, start)

    before = None
    for t in range(2):
        for e in range(2):

            def tile(n, _):
                rows = pl.ds(pl.multiple_of(n * 128, 128), 128)
                total = None
                for r in range(4):
                    dot = jnp.dot(
                        a[2 * (r // 2) + t, r % 2, rows, :], wb[e, r], preferred_element_type=jnp.float32
                    )
                    total = dot if total is None else total + dot
                part[t, e, rows, :] = total.astype(jnp.bfloat16)
                return 0

            lax.fori_loop(0, 4, tile, 0)
            if before is not None:
                pass_on(*before, True)
            before = (t, e)
    pass_on(*before, True)
    for n in range(4):
        arrived(got.at[n], r_d.at[n])

    def add(n, _):
        rows = pl.ds(pl.multiple_of(n * 64, 64), 64)
        total = got[0, rows, :].astype(jnp.float32)
        for m in range(1, 4):
            total = total + got[m, rows, :].astype(jnp.float32)
        out[rows, :] = total.astype(jnp.bfloat16)
        return 0

    lax.fori_loop(0, 8, add, 0)

    spread(False)
    lax.fori_loop(0, 4, w_sent, 0)

    @pl.when(working)
    def _():
        def sent(n, _):
            to_sibling(2 * n).wait_send()
            to_sibling(2 * n + 1).wait_send()
            to_partner(n).wait_send()
            return 0

        lax.fori_loop(0, 8, sent, 0)
        give_back(False)

    for i in range(3):
        for dx in (1, 2, 3):
            to_row(dx, i).wait_send()
        for slot in range(4):
            cross(slot, i).wait_send()
    for t in range(2):
        for e in range(2):
            pass_on(t, e, False)


W_LAG = 2


def body(queries, keys, values, frame_of_block, pair_mask, w_out):
    dma = pltpu.SemaphoreType.DMA
    wide = 3 * HD
    meta = jnp.concatenate(
        [pair_mask.reshape(-1), frame_of_block, jnp.zeros((62,), jnp.int32)]
    ).reshape(1, 128)
    return pl.pallas_call(
        kernel,
        name="frames",
        out_shape=jax.ShapeDtypeStruct((TOK, wide), jnp.bfloat16),
        in_specs=[pl.BlockSpec(memory_space=VMEM)] * 5,
        out_specs=pl.BlockSpec(memory_space=VMEM),
        scratch_shapes=[
            VMEM((4, TOK, HD), jnp.bfloat16),
            VMEM((2, 16, TOK, HD), jnp.bfloat16),
            VMEM((16, 1, 128), jnp.int32),
            pltpu.SMEM((16, 1, 128), jnp.int32),
            VMEM((2, 4, wide, wide), jnp.bfloat16),
            VMEM((4 * TOK, 2 * HD), jnp.float32),
            VMEM((4 * TOK, HD), jnp.float32),
            VMEM((4, TOK, HD), jnp.bfloat16),
            VMEM((4, 2, TOK, wide), jnp.bfloat16),
            VMEM((2, 2, TOK, wide), jnp.bfloat16),
            VMEM((4, TOK, wide), jnp.bfloat16),
            dma((3,)), dma((3, 2)), dma((3, 2, 2)), dma((16,)), dma((8,)), dma((3, 2, 4)),
            dma((4,)), dma((8,)), dma((8,)), dma((16,)), dma, dma((2, 4)), dma,
            dma((4,)), dma((4, 3)), dma((4, 3)), dma((2, 2)),
            dma((3,)), dma((4, 3)), dma((4, 3)), dma((4,)),
        ],
        compiler_params=pltpu.CompilerParams(
            collective_id=0, has_side_effects=True, vmem_limit_bytes=48 * 1024 * 1024
        ),
    )(queries, keys, values, meta, w_out)


def solution(mesh):
    return jax.shard_map(
        body,
        mesh=mesh,
        in_specs=(
            P("seq", "head"),
            P("seq", "head"),
            P("seq", "head"),
            P("seq"),
            P("seq", None),
            P("head", "seq"),
        ),
        out_specs=P("seq", "head"),
        check_vma=False,
    )
```

time: 463 us -> 159 us (0.34)
  the two profiles are of different devices: /device:TPU:27 before, /device:TPU:99 now
where the time goes in v3:
time: 159 us
  Pallas kernels  153 us (96%)
  local copies, waits for them, and re-layouts  6.11 us (4%)
    pallas_call x1, Pallas kernels, body(): pl.pallas_call(kernel, name='frames', out_shape=jax.ShapeDtypeStruct((TOK...  153 us
    unnamed x11, local copies, waits for them, and re-layouts  5.35 us

profile of v3, /device:TPU:99, one launch (start us, length us, event | category | flops | bytes accessed | tf_op | source)
XLA Modules:
  0.0 158.8 jit_solution(16960104762245256298)
XLA Ops:
  0.0 0.8 reshape.6
  0.8 0.0 copy-start.4
  0.8 0.7 copy-done.4
  1.4 0.1 add_bitcast_fusion.meta
  1.5 0.0 copy-start
  1.5 1.0 copy-done
  2.5 0.0 copy-start.1
  2.5 1.0 copy-done.1
  3.5 0.0 copy-start.2
  3.5 1.0 copy-done.2
  4.5 0.0 copy-start.3
  4.5 1.0 copy-done.3
  5.4 152.6 %frames.1 = bf16[512,384]{1,0:T(8,128)(2,1)S(1)} custom-call(bf16[512,384]{1,0:T(8,128)(2,1)S(1)} %copy-done, bf16[512,384]{1,0:T(8,128)(2,1)S(1)} %copy-done.1, bf16[512,384]{1,0:T(8,128)(2,1)S(1)} %copy-done.2, s32[1,128]{1,0:T(1,128)S(1)} %add_bitcast_fusion.meta, bf16[384,384]{1,0:T(8,128)(2,1)S(1)} %copy-done.3), custom_call_target="tpu_custom_call" | custom-call | tf_op jit(solution)/shard_map/frames/pallas_call | solution.py:377
  158.0 0.7 copy.8
  (1 shorter events, 0.0 us)
Async XLA Ops:
  0.8 0.7 copy-start.4
  1.5 1.0 copy-start
  2.5 1.0 copy-start.1
  3.5 1.0 copy-start.2
  4.5 1.0 copy-start.3

commit v4 on v3

--- a/solution.py
+++ b/solution.py
@@ -25,14 +25,15 @@
     pltpu.make_async_copy(ref, ref, sem).wait()
 
 
-def chunk_owner(kk, j):
-    return jnp.where(j == 0, kk, jnp.where(j == 1, 7 - kk, jnp.where(j == 2, 8 + kk, 15 - kk)))
+def chunk_owner(c, x_lo, j):
+    flip = lax.rem(j, 2)
+    return 2 * (2 * j + jnp.where(flip == 1, 1 - c, c)) + x_lo
 
 
 def kernel(
-    q, k, v, meta, w, out,
-    qb, kv, mt, table, wb, acc, peak, ob, a, part, got,
-    s_q, s_kv, s_m, s_f, s_p, s_w, r_q, r_z, r_x, r_s, r_m, r_w, r_t,
+    q, k, v, frame, pair, w, out,
+    meta, mask, own, qb, kv, mt, table, wb, acc, peak, ob, a, part, got,
+    s_l, s_q, s_kv, s_m, s_f, s_p, s_w, r_q, r_z, r_x, r_s, r_m, r_w, r_t,
     s_o, s_a, s_b, s_d, r_o, r_a, r_b, r_d,
 ):
     s, h = lax.axis_index("seq"), lax.axis_index("head")
@@ -41,10 +42,14 @@
     z, x_lo = s // 2, lax.rem(s, 2)
     y, x_hi = hb // 4, lax.rem(hb, 4) // 2
     x = 2 * x_hi + x_lo
-    kk = 2 * c + x_lo
     third = lax.rem(z, 4)
     working = third < 3
     barrier = pltpu.get_barrier_semaphore()
+
+    load_mask = pltpu.make_async_copy(pair, mask, s_l.at[0])
+    load_frame = pltpu.make_async_copy(frame, own, s_l.at[1])
+    load_mask.start()
+    load_frame.start()
 
     def greet(seq, head):
         pl.semaphore_signal(barrier, inc=1, device_id=(seq, head), device_id_type=MESH)
@@ -70,6 +75,12 @@
     lax.fori_loop(0, 32, greet_group, 0)
     lax.fori_loop(0, 4, greet_row, 0)
     lax.fori_loop(0, 12, greet_line, 0)
+    load_mask.wait()
+    load_frame.wait()
+    lane = lax.broadcasted_iota(jnp.int32, (1, 32), 1)
+    meta[0:1, 0:32] = mask[0:1, :]
+    meta[0:1, 32:64] = mask[1:2, :]
+    meta[0:1, 64:96] = jnp.where(lane == 0, own[0], own[1])
     pl.semaphore_wait(barrier, 47)
 
     def put(src, dst, send, recv, seq, head, start):
@@ -93,29 +104,39 @@
     def cols(i):
         return pl.ds(i * HD, HD)
 
-    rising = lax.rem(z - 4 * c + 9, 8) < 2
-    low = lax.rem(s, 8)
-    worker = jnp.where(low < 4, low, 7 - low)
-
-    def spread(start):
+    off = lax.rem(z - 4 * c + 8, 8)
+
+    def order(r):
+        rising = jnp.where((off == 0) | (off > 5), r, 2 - r)
+        return jnp.where(off == 1, jnp.where(r == 0, 1, jnp.where(r == 1, 0, 2)), jnp.where(off == 5, jnp.where(r == 0, 0, 3 - r), rising))
+
+    worker = lax.rem((z + 1) // 2, 2)
+
+    def spread_meta(start):
         for r in range(3):
-            i = jnp.where(rising | (z == 4 * c + 6 - 8 * c), r, 2 - r)
-            pz = 4 * c + i
-            lanes = pl.ds(pl.multiple_of(i * HD, HD), HD)
-            put(q.at[:, lanes], qb.at[s // 4], s_q.at[r], r_q.at[s // 4], 2 * pz + lax.rem(worker, 2), hb + worker // 2, start)
-        for r in range(3):
-            i = jnp.where(rising | (z == 4 * c + 6 - 8 * c), r, 2 - r)
-            pz = 4 * c + i
-            lanes = pl.ds(pl.multiple_of(i * HD, HD), HD)
+            pz = 4 * c + order(r)
             for px in range(2):
                 for pc in range(2):
                     put(meta, mt.at[s], s_m.at[r, px, pc], r_m, 2 * pz + px, hb + pc, start)
-            for t, src in ((0, k), (1, v)):
-                put(src.at[:, lanes], kv.at[t, s], s_kv.at[r, t], r_z.at[z], 2 * pz + x_lo, hb + t, start)
+
+    def spread(r, start):
+        i = order(r)
+        lanes = pl.ds(pl.multiple_of(i * HD, HD), HD)
+        seq = 2 * (4 * c + i) + x_lo
+        put(q.at[:, lanes], qb.at[z // 2], s_q.at[r], r_q.at[z // 2], seq, hb + worker, start)
+        for t, src in ((0, k), (1, v)):
+            put(src.at[:, lanes], kv.at[t, s], s_kv.at[r, t], r_z.at[z], seq, hb + t, start)
+
+    def spread_w(start):
         e, r = lax.rem(z, 4) // 2, 2 * x_hi + c
-        put(w, wb.at[e, r], s_w.at[2, 0, 0], r_w.at[e, r], s, 4 * y + 2 * lax.rem(z, 2) + z // 4, start)
-
-    spread(True)
+        put(w, wb.at[e, r], s_w.at[4, 0, 0], r_w.at[e, r], s, 4 * y + 2 * lax.rem(z, 2) + z // 4, start)
+
+    spread_meta(True)
+    spread(0, True)
+    spread_w(True)
+    if not THROTTLE:
+        spread(1, True)
+        spread(2, True)
 
     def source_at(n):
         far = (n + 1) // 2
@@ -128,43 +149,41 @@
         piece = 2 * zs + x_lo
         return remote(kv.at[c, piece], kv.at[c, piece], s_p.at[zs], r_x.at[zs], 2 * z + 1 - x_lo, h)
 
-    def w_hop(e, r, up):
-        to = lax.rem(z + (1 if up else 7), 8)
-        return remote(wb.at[e, r], wb.at[e, r], s_w.at[1 if up else 0, e, r], r_w.at[e, r], 2 * to + x_lo, h)
-
-    def w_far(e):
-        return lax.rem(z - (4 * c + 2 * e + x_hi) + 8, 8)
-
-    def w_turn(n):
+    def w_hop(e, r, to, slot):
+        return remote(wb.at[e, r], wb.at[e, r], s_w.at[slot, e, r], r_w.at[e, r], 2 * lax.rem(z + to, 8) + x_lo, h)
+
+    def w_each(source, relay, do):
         for e in range(2):
-            far = w_far(e)
-            r = n - jnp.where(far > 4, 8 - far, far)
-
-            @pl.when((r >= 0) & (r < 4))
-            def _():
-                arrived(wb.at[e, r], r_w.at[e, r])
-
-                @pl.when(far < 4)
-                def _():
-                    w_hop(e, r, True).start()
-
-                @pl.when((far == 0) | (far > 5))
-                def _():
-                    w_hop(e, r, False).start()
-
-    def w_sent(r, _):
+            far = lax.rem(z - (4 * c + 2 * e + x_hi) + 8, 8)
+            for at, reach in ((0, (1, 7, 2, 6)), (2, (1, 2)), (6, (7,))):
+                if source if at == 0 else relay:
+
+                    @pl.when(far == at)
+                    def _(e=e, reach=reach):
+                        do(e, reach)
+
+    def w_start(e, reach):
+        for r in range(4):
+            arrived(wb.at[e, r], r_w.at[e, r])
+            for slot, to in enumerate(reach):
+                w_hop(e, r, to, slot).start()
+
+    def w_sent(e, reach):
+        for r in range(4):
+            for slot, to in enumerate(reach):
+                w_hop(e, r, to, slot).wait_send()
+
+    def w_end(e, reach):
+        for r in range(4):
+            arrived(wb.at[e, r], r_w.at[e, r])
+
+    def w_rest():
         for e in range(2):
-            far = w_far(e)
-
-            @pl.when(far < 4)
-            def _():
-                w_hop(e, r, True).wait_send()
-
-            @pl.when((far == 0) | (far > 5))
-            def _():
-                w_hop(e, r, False).wait_send()
-
-        return 0
+            far = lax.rem(z - (4 * c + 2 * e + x_hi) + 8, 8)
+
+            @pl.when((far != 0) & (far != 2) & (far != 6))
+            def _(e=e):
+                w_end(e, ())
 
     def attend(piece, j, owner):
         keys = [kv[0, piece, pl.ds(u * BLK, BLK), :] for u in range(2)]
@@ -211,6 +230,21 @@
         peak[...] = jnp.full_like(peak, -1e30)
 
     def turn(n, _):
+        for r in range(2 if THROTTLE else 0):
+
+            @pl.when(n == THROTTLE + r)
+            def _(r=r):
+                spread(r, False)
+                spread(r + 1, True)
+
+        @pl.when(n == W_FROM)
+        def _():
+            w_each(True, False, w_start)
+
+        @pl.when(n == W_RELAY)
+        def _():
+            w_each(False, True, w_start)
+
         @pl.when(working & (n < 8))
         def _():
             zs = source_at(n)
@@ -226,14 +260,8 @@
             arrived(kv.at[c, piece], r_x.at[zs])
             to_sibling(piece).start()
 
-        @pl.when(n >= W_LAG)
-        def _():
-            w_turn(n - W_LAG)
-
         @pl.when(working & (n == 2))
         def _():
-            for j in range(4):
-                arrived(qb.at[j], r_q.at[j])
             arrived(mt, r_m)
             local = pltpu.make_async_copy(mt, table, r_t)
             local.start()
@@ -241,45 +269,64 @@
 
         @pl.when(working & (n > 1) & (n < 10))
         def _():
-            zs = source_at(n - 2)
+            fresh = n - 2
+            zs = source_at(fresh)
             for side in range(2):
                 piece = 2 * zs + side
                 arrived(kv.at[1 - c, piece], r_s.at[piece])
 
-            def one(m, _):
-                piece, j = 2 * zs + m // 4, lax.rem(m, 4)
-                owner = chunk_owner(kk, j)
-
-                @pl.when(piece <= owner + 2)
+            def chunk(j, _):
+                owner = chunk_owner(c, x_lo, j)
+                away = lax.rem(owner // 2 - z + 8, 8)
+                since = jnp.where(away == 0, 0, jnp.where(away < 5, 2 * away - 1, 16 - 2 * away))
+
+                @pl.when(since == fresh)
                 def _():
-                    attend(piece, j, owner)
-
+                    arrived(qb.at[j], r_q.at[j])
+
+                def one(m, _):
+                    piece = 2 * source_at(m // 2) + lax.rem(m, 2)
+
+                    @pl.when(piece <= owner + 2)
+                    def _():
+                        attend(piece, j, owner)
+
+                    return 0
+
+                first = jnp.where(since < fresh, fresh, jnp.where(since == fresh, 0, fresh + 1))
+                lax.fori_loop(2 * first, 2 * fresh + 2, one, 0)
                 return 0
 
-            lax.fori_loop(0, 8, one, 0)
+            lax.fori_loop(0, 4, chunk, 0)
 
         return 0
 
-    lax.fori_loop(0, max(10, 8 + W_LAG), turn, 0)
-
-    def give_back(start):
+    lax.fori_loop(0, 10, turn, 0)
+
+    def give_back(j, start):
         lanes = pl.ds(pl.multiple_of(third * HD, HD), HD)
-        for j in range(4):
-            to = chunk_owner(kk, j)
-            slot = 2 * x_hi + lax.rem(to, 2)
-            put(ob.at[j], a.at[slot, z // 4, :, lanes], s_o.at[j], r_o.at[third], to, hb + z // 4, start)
+        put(ob.at[j], a.at[x, z // 4, :, lanes], s_o.at[j], r_o.at[third], chunk_owner(c, x_lo, j), hb + z // 4, start)
 
     @pl.when(working)
     def _():
-        def finish(n, _):
-            rows = pl.ds(pl.multiple_of(n * 128, 128), 128)
-            ob[n // 4, pl.ds(pl.multiple_of(lax.rem(n, 4) * 128, 128), 128), :] = (
-                acc[rows, :HD] / acc[rows, HD:]
-            ).astype(jnp.bfloat16)
-            return 0
-
-        lax.fori_loop(0, 16, finish, 0)
-        give_back(True)
+        for j in range(4):
+
+            def finish(n, _):
+                rows = pl.ds(pl.multiple_of(j * TOK + n * 128, 128), 128)
+                ob[j, pl.ds(pl.multiple_of(n * 128, 128), 128), :] = (acc[rows, :HD] / acc[rows, HD:]).astype(
+                    jnp.bfloat16
+                )
+                return 0
+
+            lax.fori_loop(0, 4, finish, 0)
+            if j > 0:
+                give_back(j - 1, True)
+        give_back(3, True)
+
+    if W_FROM > 9:
+        w_each(True, False, w_start)
+    if W_RELAY == 10:
+        w_each(False, True, w_start)
 
     def cross(slot, i):
         piece = a.at[slot, c, :, cols(i)]
@@ -292,24 +339,33 @@
 
     for i in range(3):
         arrived(a.at[x, c, :, cols(i)], r_o.at[i])
-        for dx in (1, 3, 2):
+        for dx in (1, 3):
             to_row(dx, i).start()
         cross(x, i).start()
     for i in range(3):
-        for dx in (3, 1, 2):
+        to_row(2, i).start()
+    if W_RELAY > 10:
+        w_each(False, True, w_start)
+    w_rest()
+
+    def gather(far):
+        for i in range(3):
+            for dx in far:
+                slot = lax.rem(x + dx, 4)
+                arrived(a.at[slot, c, :, cols(i)], r_a.at[slot, i])
+                cross(slot, i).start()
+
+    def gathered(far):
+        for dx in far:
             slot = lax.rem(x + dx, 4)
-            arrived(a.at[slot, c, :, cols(i)], r_a.at[slot, i])
-            cross(slot, i).start()
-    for slot in range(4):
-        for i in range(3):
-            arrived(a.at[slot, 1 - c, :, cols(i)], r_b.at[slot, i])
+            for i in range(3):
+                arrived(a.at[slot, 1 - c, :, cols(i)], r_b.at[slot, i])
 
     def pass_on(t, e, start):
         py = 2 * c + e
         put(part.at[t, e], got.at[y], s_d.at[t, e], r_d.at[y], 2 * z + t, 4 * py + 2 * x_hi + x_lo, start)
 
-    before = None
-    for t in range(2):
+    def multiply(t):
         for e in range(2):
 
             def tile(n, _):
@@ -324,10 +380,16 @@
                 return 0
 
             lax.fori_loop(0, 4, tile, 0)
-            if before is not None:
-                pass_on(*before, True)
-            before = (t, e)
-    pass_on(*before, True)
+            if e == 1:
+                pass_on(t, 0, True)
+        pass_on(t, 1, True)
+
+    gather((3, 1))
+    gathered((3, 1))
+    multiply(1 - x_lo)
+    gather((2,))
+    gathered((2, 0))
+    multiply(x_lo)
     for n in range(4):
         arrived(got.at[n], r_d.at[n])
 
@@ -341,8 +403,11 @@
 
     lax.fori_loop(0, 8, add, 0)
 
-    spread(False)
-    lax.fori_loop(0, 4, w_sent, 0)
+    spread_meta(False)
+    spread_w(False)
+    for r in range(2 if THROTTLE else 0, 3):
+        spread(r, False)
+    w_each(True, True, w_sent)
 
     @pl.when(working)
     def _():
@@ -353,7 +418,8 @@
             return 0
 
         lax.fori_loop(0, 8, sent, 0)
-        give_back(False)
+        for j in range(4):
+            give_back(j, False)
 
     for i in range(3):
         for dx in (1, 2, 3):
@@ -365,22 +431,24 @@
             pass_on(t, e, False)
 
 
-W_LAG = 2
+W_FROM = 4
+W_RELAY = 10
+THROTTLE = 1
 
 
 def body(queries, keys, values, frame_of_block, pair_mask, w_out):
     dma = pltpu.SemaphoreType.DMA
     wide = 3 * HD
-    meta = jnp.concatenate(
-        [pair_mask.reshape(-1), frame_of_block, jnp.zeros((62,), jnp.int32)]
-    ).reshape(1, 128)
     return pl.pallas_call(
         kernel,
         name="frames",
         out_shape=jax.ShapeDtypeStruct((TOK, wide), jnp.bfloat16),
-        in_specs=[pl.BlockSpec(memory_space=VMEM)] * 5,
+        in_specs=[pl.BlockSpec(memory_space=pl.ANY)] * 6,
         out_specs=pl.BlockSpec(memory_space=VMEM),
         scratch_shapes=[
+            VMEM((1, 128), jnp.int32),
+            VMEM((2, 32), jnp.int32),
+            pltpu.SMEM((2,), jnp.int32),
             VMEM((4, TOK, HD), jnp.bfloat16),
             VMEM((2, 16, TOK, HD), jnp.bfloat16),
             VMEM((16, 1, 128), jnp.int32),
@@ -392,15 +460,15 @@
             VMEM((4, 2, TOK, wide), jnp.bfloat16),
             VMEM((2, 2, TOK, wide), jnp.bfloat16),
             VMEM((4, TOK, wide), jnp.bfloat16),
-            dma((3,)), dma((3, 2)), dma((3, 2, 2)), dma((16,)), dma((8,)), dma((3, 2, 4)),
+            dma((2,)), dma((3,)), dma((3, 2)), dma((3, 2, 2)), dma((16,)), dma((8,)), dma((5, 2, 4)),
             dma((4,)), dma((8,)), dma((8,)), dma((16,)), dma, dma((2, 4)), dma,
             dma((4,)), dma((4, 3)), dma((4, 3)), dma((2, 2)),
             dma((3,)), dma((4, 3)), dma((4, 3)), dma((4,)),
         ],
         compiler_params=pltpu.CompilerParams(
-            collective_id=0, has_side_effects=True, vmem_limit_bytes=48 * 1024 * 1024
+            collective_id=0, has_side_effects=True, vmem_limit_bytes=67_000_000
         ),
-    )(queries, keys, values, meta, w_out)
+    )(queries, keys, values, frame_of_block, pair_mask, w_out)
 
 
 def solution(mesh):

time: 159 us -> 147 us (0.925)
  the two profiles are of different devices: /device:TPU:99 before, /device:TPU:75 now
where the time goes in v4:
time: 147 us
  Pallas kernels  145 us (99%)
  local copies, waits for them, and re-layouts  1.78 us (1%)
    pallas_call x1, Pallas kernels, body(): pl.pallas_call(kernel, name='frames', out_shape=jax.ShapeDtypeStruct((TOK...  145 us

profile of v4, /device:TPU:75, one launch (start us, length us, event | category | flops | bytes accessed | tf_op | source)
XLA Modules:
  0.0 147.0 jit_solution(4399408753849140571)
XLA Ops:
  0.0 145.2 %frames.1 = bf16[512,384]{1,0:T(8,128)(2,1)} custom-call(bf16[512,384]{1,0:T(8,128)(2,1)} %q.1, bf16[512,384]{1,0:T(8,128)(2,1)} %k.1, bf16[512,384]{1,0:T(8,128)(2,1)} %v.1, s32[2]{0:T(128)} %frame.1, s32[2,32]{1,0:T(2,128)} %pair.1, bf16[384,384]{1,0:T(8,128)(2,1)} %w.1), custom_call_target="tpu_custom_call" | custom-call | tf_op jit(solution)/shard_map/frames/pallas_call | solution.py:442
  145.2 1.8 %copy.8 = bf16[512,384]{1,0:T(8,128)(2,1)} copy(bf16[512,384]{1,0:T(8,128)(2,1)} %frames.1) | data formatting | bytes 786432

commit v5 on v4

--- a/solution.py
+++ b/solution.py
@@ -120,7 +120,7 @@
                     put(meta, mt.at[s], s_m.at[r, px, pc], r_m, 2 * pz + px, hb + pc, start)
 
     def spread(r, start):
-        i = order(r)
+        i = order(2 - r if FAR_SEND else r)
         lanes = pl.ds(pl.multiple_of(i * HD, HD), HD)
         seq = 2 * (4 * c + i) + x_lo
         put(q.at[:, lanes], qb.at[z // 2], s_q.at[r], r_q.at[z // 2], seq, hb + worker, start)
@@ -139,6 +139,9 @@
         spread(2, True)
 
     def source_at(n):
+        if FAR_FIRST:
+            far = 4 - n // 2
+            return lax.rem(z + jnp.where(n == 0, 0, jnp.where(lax.rem(n, 2) == 0, far, 8 - far)), 8)
         far = (n + 1) // 2
         return lax.rem(z + jnp.where(lax.rem(n, 2) == 1, far, 8 - far), 8)
 
@@ -189,40 +192,53 @@
         keys = [kv[0, piece, pl.ds(u * BLK, BLK), :] for u in range(2)]
         ones = jnp.ones((BLK, HD), jnp.bfloat16)
         wide = [jnp.concatenate([kv[1, piece, pl.ds(u * BLK, BLK), :], ones], axis=1) for u in range(2)]
-        for tile in range(4):
-            half = tile // 2
-            ok = []
-            for u in range(2):
-                near = (table[owner, 0, 32 * half + 2 * piece + u] == 1) & (2 * piece + u <= 2 * owner + half)
-                ok.append(near | (table[piece, 0, 64 + u] == table[owner, 0, 64 + half]))
-            rows = pl.ds(tile * 128, 128)
-            held = pl.ds(pl.multiple_of(j * TOK + tile * 128, 128), 128)
-            query = qb[j, rows, :]
-            score = [
-                lax.dot_general(query, keys[u], (((1,), (1,)), ((), ())), preferred_element_type=jnp.float32)
+        ok = [
+            [
+                ((table[owner, 0, 32 * half + 2 * piece + u] == 1) & (2 * piece + u <= 2 * owner + half))
+                | (table[piece, 0, 64 + u] == table[owner, 0, 64 + half])
                 for u in range(2)
             ]
+            for half in range(2)
+        ]
+        held = [pl.ds(pl.multiple_of(j * TOK + tile * 128, 128), 128) for tile in range(4)]
+        scores = []
+        for tile in range(4):
+            query = qb[j, pl.ds(tile * 128, 128), :]
+            scores.append(
+                [
+                    lax.dot_general(query, keys[u], (((1,), (1,)), ((), ())), preferred_element_type=jnp.float32)
+                    for u in range(2)
+                ]
+            )
+        weights = []
+        for tile in range(4):
+            score, seen = scores[tile], ok[tile // 2]
             tops = [
-                jnp.maximum(score[u][:, :HD], score[u][:, HD:]) + jnp.where(ok[u], 0.0, -1e30) for u in range(2)
+                jnp.maximum(score[u][:, :HD], score[u][:, HD:]) + jnp.where(seen[u], 0.0, -1e30) for u in range(2)
             ]
-            old = peak[held, :]
+            old = peak[held[tile], :]
             new = jnp.maximum(old, jnp.max(jnp.maximum(tops[0], tops[1]), axis=1, keepdims=True))
-            peak[held, :] = new
-            shrink = jnp.exp2((old - new) * FACTOR)
-            added = None
+            peak[held[tile], :] = new
+            row = []
             for u in range(2):
-                base = jnp.where(ok[u], new, 1e30)
-                weight = jnp.concatenate(
-                    [
-                        jnp.exp2((score[u][:, cols_] - base) * FACTOR).astype(jnp.bfloat16)
-                        for cols_ in (slice(0, HD), slice(HD, 2 * HD))
-                    ],
-                    axis=1,
+                base = jnp.where(seen[u], new, 1e30)
+                row.append(
+                    jnp.concatenate(
+                        [
+                            jnp.exp2((score[u][:, lanes] - base) * FACTOR).astype(jnp.bfloat16)
+                            for lanes in (slice(0, HD), slice(HD, 2 * HD))
+                        ],
+                        axis=1,
+                    )
                 )
-                dot = jnp.dot(weight, wide[u], preferred_element_type=jnp.float32)
-                added = dot if added is None else added + dot
-            acc[held, :HD] = acc[held, :HD] * shrink + added[:, :HD]
-            acc[held, HD:] = acc[held, HD:] * shrink + added[:, HD:]
+            weights.append((row, jnp.exp2((old - new) * FACTOR)))
+        for tile in range(4):
+            row, shrink = weights[tile]
+            added = jnp.dot(row[0], wide[0], preferred_element_type=jnp.float32) + jnp.dot(
+                row[1], wide[1], preferred_element_type=jnp.float32
+            )
+            acc[held[tile], :HD] = acc[held[tile], :HD] * shrink + added[:, :HD]
+            acc[held[tile], HD:] = acc[held[tile], HD:] * shrink + added[:, HD:]
 
     @pl.when(working)
     def _():
@@ -278,7 +294,10 @@
             def chunk(j, _):
                 owner = chunk_owner(c, x_lo, j)
                 away = lax.rem(owner // 2 - z + 8, 8)
-                since = jnp.where(away == 0, 0, jnp.where(away < 5, 2 * away - 1, 16 - 2 * away))
+                if FAR_FIRST:
+                    since = jnp.where(away == 0, 0, jnp.where(away < 4, 8 - 2 * away, 2 * away - 7))
+                else:
+                    since = jnp.where(away == 0, 0, jnp.where(away < 5, 2 * away - 1, 16 - 2 * away))
 
                 @pl.when(since == fresh)
                 def _():
@@ -346,7 +365,6 @@
         to_row(2, i).start()
     if W_RELAY > 10:
         w_each(False, True, w_start)
-    w_rest()
 
     def gather(far):
         for i in range(3):
@@ -385,9 +403,10 @@
         pass_on(t, 1, True)
 
     gather((3, 1))
+    gather((2,))
+    w_rest()
     gathered((3, 1))
     multiply(1 - x_lo)
-    gather((2,))
     gathered((2, 0))
     multiply(x_lo)
     for n in range(4):
@@ -433,7 +452,9 @@
 
 W_FROM = 4
 W_RELAY = 10
-THROTTLE = 1
+THROTTLE = 0
+FAR_SEND = True
+FAR_FIRST = True
 
 
 def body(queries, keys, values, frame_of_block, pair_mask, w_out):

time: 147 us -> 139 us (0.946)
  the two profiles are of different devices: /device:TPU:75 before, /device:TPU:27 now
where the time goes in v5:
time: 139 us; the launch traced here: 137 us
  Pallas kernels  136 us (98%)
  local copies, waits for them, and re-layouts  1.78 us (1%)
    pallas_call x1, Pallas kernels, body(): pl.pallas_call(kernel, name='frames', out_shape=jax.ShapeDtypeStruct((TOK...  136 us

profile of v5, /device:TPU:27, one launch (start us, length us, event | category | flops | bytes accessed | tf_op | source)
XLA Modules:
  0.0 137.3 jit_solution(1239157003240105549)
XLA Ops:
  0.0 135.5 %frames.1 = bf16[512,384]{1,0:T(8,128)(2,1)} custom-call(bf16[512,384]{1,0:T(8,128)(2,1)} %q.1, bf16[512,384]{1,0:T(8,128)(2,1)} %k.1, bf16[512,384]{1,0:T(8,128)(2,1)} %v.1, s32[2]{0:T(128)} %frame.1, s32[2,32]{1,0:T(2,128)} %pair.1, bf16[384,384]{1,0:T(8,128)(2,1)} %w.1), custom_call_target="tpu_custom_call" | custom-call | tf_op jit(solution)/shard_map/frames/pallas_call | solution.py:463
  135.5 1.8 %copy.8 = bf16[512,384]{1,0:T(8,128)(2,1)} copy(bf16[512,384]{1,0:T(8,128)(2,1)} %frames.1) | data formatting | bytes 786432

commit v6 on v5

--- a/solution.py
+++ b/solution.py
@@ -253,6 +253,11 @@
                 spread(r, False)
                 spread(r + 1, True)
 
+        @pl.when((n == W_FROM) & jnp.logical_not(working))
+        def _():
+            for r in range(2 if THROTTLE else 0, 3):
+                spread(r, False)
+
         @pl.when(n == W_FROM)
         def _():
             w_each(True, False, w_start)
@@ -356,13 +361,20 @@
         piece = a.at[x, c, :, cols(i)]
         return remote(piece, piece, s_a.at[dx, i], r_a.at[x, i], 2 * z + lax.rem(px, 2), 4 * y + 2 * (px // 2) + c)
 
+    def relay(i):
+        right = i + c < 2
+        slot = lax.rem(jnp.where(right, x + 3, x + 1), 4)
+        px = lax.rem(jnp.where(right, x + 1, x + 3), 4)
+        piece = a.at[slot, c, :, cols(i)]
+        return remote(
+            piece, piece, s_a.at[2, i], r_a.at[slot, i], 2 * z + lax.rem(px, 2), 4 * y + 2 * (px // 2) + c
+        )
+
     for i in range(3):
         arrived(a.at[x, c, :, cols(i)], r_o.at[i])
         for dx in (1, 3):
             to_row(dx, i).start()
         cross(x, i).start()
-    for i in range(3):
-        to_row(2, i).start()
     if W_RELAY > 10:
         w_each(False, True, w_start)
 
@@ -371,6 +383,12 @@
             for dx in far:
                 slot = lax.rem(x + dx, 4)
                 arrived(a.at[slot, c, :, cols(i)], r_a.at[slot, i])
+                if dx != 2:
+
+                    @pl.when((i + c < 2) if dx == 3 else (i + c > 1))
+                    def _():
+                        relay(i).start()
+
                 cross(slot, i).start()
 
     def gathered(far):
@@ -387,7 +405,7 @@
         for e in range(2):
 
             def tile(n, _):
-                rows = pl.ds(pl.multiple_of(n * 128, 128), 128)
+                rows = pl.ds(pl.multiple_of(n * M_TILE, M_TILE), M_TILE)
                 total = None
                 for r in range(4):
                     dot = jnp.dot(
@@ -397,7 +415,7 @@
                 part[t, e, rows, :] = total.astype(jnp.bfloat16)
                 return 0
 
-            lax.fori_loop(0, 4, tile, 0)
+            lax.fori_loop(0, TOK // M_TILE, tile, 0)
             if e == 1:
                 pass_on(t, 0, True)
         pass_on(t, 1, True)
@@ -424,8 +442,12 @@
 
     spread_meta(False)
     spread_w(False)
-    for r in range(2 if THROTTLE else 0, 3):
-        spread(r, False)
+
+    @pl.when(working)
+    def _():
+        for r in range(2 if THROTTLE else 0, 3):
+            spread(r, False)
+
     w_each(True, True, w_sent)
 
     @pl.when(working)
@@ -441,8 +463,9 @@
             give_back(j, False)
 
     for i in range(3):
-        for dx in (1, 2, 3):
+        for dx in (1, 3):
             to_row(dx, i).wait_send()
+        relay(i).wait_send()
         for slot in range(4):
             cross(slot, i).wait_send()
     for t in range(2):
@@ -451,6 +474,7 @@
 
 
 W_FROM = 4
+M_TILE = 512
 W_RELAY = 10
 THROTTLE = 0
 FAR_SEND = True

time: 139 us -> 136 us (0.978)
  Pallas kernels: 136 us -> 134 us
    pallas_call x1, Pallas kernels: 136 us -> 134 us  [body(): pl.pallas_call(kernel, name='frames', out_shape=jax.ShapeDtypeStruct((TOK...]
where the time goes in v6:
time: 136 us; the launch traced here: 135 us
  Pallas kernels  134 us (99%)
  local copies, waits for them, and re-layouts  1.78 us (1%)
    pallas_call x1, Pallas kernels, body(): pl.pallas_call(kernel, name='frames', out_shape=jax.ShapeDtypeStruct((TOK...  134 us

profile of v6, /device:TPU:27, one launch (start us, length us, event | category | flops | bytes accessed | tf_op | source)
XLA Modules:
  0.0 135.4 jit_solution(14445003010293753936)
XLA Ops:
  0.0 133.6 %frames.1 = bf16[512,384]{1,0:T(8,128)(2,1)} custom-call(bf16[512,384]{1,0:T(8,128)(2,1)} %q.1, bf16[512,384]{1,0:T(8,128)(2,1)} %k.1, bf16[512,384]{1,0:T(8,128)(2,1)} %v.1, s32[2]{0:T(128)} %frame.1, s32[2,32]{1,0:T(2,128)} %pair.1, bf16[384,384]{1,0:T(8,128)(2,1)} %w.1), custom_call_target="tpu_custom_call" | custom-call | tf_op jit(solution)/shard_map/frames/pallas_call | solution.py:487
  133.6 1.8 %copy.8 = bf16[512,384]{1,0:T(8,128)(2,1)} copy(bf16[512,384]{1,0:T(8,128)(2,1)} %frames.1) | data formatting | bytes 786432

commit v7 on v6

--- a/solution.py
+++ b/solution.py
@@ -180,13 +180,12 @@
         for r in range(4):
             arrived(wb.at[e, r], r_w.at[e, r])
 
-    def w_rest():
-        for e in range(2):
-            far = lax.rem(z - (4 * c + 2 * e + x_hi) + 8, 8)
-
-            @pl.when((far != 0) & (far != 2) & (far != 6))
-            def _(e=e):
-                w_end(e, ())
+    def w_rest(e):
+        far = lax.rem(z - (4 * c + 2 * e + x_hi) + 8, 8)
+
+        @pl.when((far != 0) & (far != 2) & (far != 6))
+        def _():
+            w_end(e, ())
 
     def attend(piece, j, owner):
         keys = [kv[0, piece, pl.ds(u * BLK, BLK), :] for u in range(2)]
@@ -401,32 +400,34 @@
         py = 2 * c + e
         put(part.at[t, e], got.at[y], s_d.at[t, e], r_d.at[y], 2 * z + t, 4 * py + 2 * x_hi + x_lo, start)
 
-    def multiply(t):
-        for e in range(2):
-
-            def tile(n, _):
-                rows = pl.ds(pl.multiple_of(n * M_TILE, M_TILE), M_TILE)
-                total = None
-                for r in range(4):
-                    dot = jnp.dot(
-                        a[2 * (r // 2) + t, r % 2, rows, :], wb[e, r], preferred_element_type=jnp.float32
-                    )
-                    total = dot if total is None else total + dot
-                part[t, e, rows, :] = total.astype(jnp.bfloat16)
-                return 0
-
-            lax.fori_loop(0, TOK // M_TILE, tile, 0)
-            if e == 1:
-                pass_on(t, 0, True)
-        pass_on(t, 1, True)
+    def multiply(t, e):
+        def tile(n, _):
+            rows = pl.ds(pl.multiple_of(n * M_TILE, M_TILE), M_TILE)
+            total = None
+            for r in range(4):
+                dot = jnp.dot(
+                    a[2 * (r // 2) + t, r % 2, rows, :], wb[e, r], preferred_element_type=jnp.float32
+                )
+                total = dot if total is None else total + dot
+            part[t, e, rows, :] = total.astype(jnp.bfloat16)
+            return 0
+
+        lax.fori_loop(0, TOK // M_TILE, tile, 0)
 
     gather((3, 1))
     gather((2,))
-    w_rest()
+    w_rest(0)
     gathered((3, 1))
-    multiply(1 - x_lo)
+    multiply(1 - x_lo, 0)
     gathered((2, 0))
-    multiply(x_lo)
+    multiply(x_lo, 0)
+    pass_on(1 - x_lo, 0, True)
+    w_rest(1)
+    pass_on(x_lo, 0, True)
+    multiply(1 - x_lo, 1)
+    multiply(x_lo, 1)
+    pass_on(1 - x_lo, 1, True)
+    pass_on(x_lo, 1, True)
     for n in range(4):
         arrived(got.at[n], r_d.at[n])
 

time: 136 us -> 136 us (level)
  no operation moved by 1% of the time
where the time goes in v7:
time: 136 us
  Pallas kernels  134 us (99%)
  local copies, waits for them, and re-layouts  1.78 us (1%)
    pallas_call x1, Pallas kernels, body(): pl.pallas_call(kernel, name='frames', out_shape=jax.ShapeDtypeStruct((TOK...  134 us

profile of v7, /device:TPU:27, one launch (start us, length us, event | category | flops | bytes accessed | tf_op | source)
XLA Modules:
  0.0 136.0 jit_solution(11114529073782701348)
XLA Ops:
  0.0 134.2 %frames.1 = bf16[512,384]{1,0:T(8,128)(2,1)} custom-call(bf16[512,384]{1,0:T(8,128)(2,1)} %q.1, bf16[512,384]{1,0:T(8,128)(2,1)} %k.1, bf16[512,384]{1,0:T(8,128)(2,1)} %v.1, s32[2]{0:T(128)} %frame.1, s32[2,32]{1,0:T(2,128)} %pair.1, bf16[384,384]{1,0:T(8,128)(2,1)} %w.1), custom_call_target="tpu_custom_call" | custom-call | tf_op jit(solution)/shard_map/frames/pallas_call | solution.py:488
  134.2 1.8 %copy.8 = bf16[512,384]{1,0:T(8,128)(2,1)} copy(bf16[512,384]{1,0:T(8,128)(2,1)} %frames.1) | data formatting | bytes 786432
